TPU v7x, 32 devices: a whole 2x2x4 slice. The times are simulated.
32 devices in a mesh: tm: 8 (over z, x), space: 4 (over y, core).
Axes of the slice: x: 2, y: 2, z: 4, core: 2. Of those that a mesh axis runs over, the one named last changes fastest.
Arguments:
- state: float32 [32, 16, 64, 128], P('tm', 'space'), may hold values from -6 to 6
- source: float32 [32, 16, 64, 128], P('tm', 'space'), may hold values from -6 to 6
- absorption: float32 [16, 64, 128], P('space'), may hold values from 0.05 to 0.5
Outputs:
- relaxed: float32 [32, 16, 64, 128], P('tm', 'space')
- coarse_residual: float32 [8, 16, 64, 128], P('tm', 'space')
- residual_norm: float32 [], replicated
All inputs are finite; a program needn't handle non-finite values.
Results may differ from a plain program's by a relative error of at most 0.0004.
Values sent between devices are 32-bit elements; how exact they have to be, the bound alone decides.
No kernel may reach another device: no remote copies, remote signals or barrier semaphores. Data moves between devices by JAX's collectives and lax.ppermute only.
A program may use at most 64 MiB of HBM per device.

v0:
```python
import math

import jax
import jax.numpy as jnp
from jax import lax
from jax.sharding import PartitionSpec as P

CF = 4
SWEEPS = 5


coupling = 4.0


def shifted(value, axis, by):
    count = lax.axis_size(axis)
    pairs = [(i, i + by) for i in range(count) if 0 <= i + by < count]
    return lax.ppermute(value, axis, pairs)


def sweep_weights(count):
    spread = 6.0 * coupling / (1.0 + 6.0 * coupling)
    return [
        1.0 / (1.0 + spread * math.cos(math.pi * (2 * k + 1) / (2 * count))) for k in range(count)
    ]


def apply_inner(extended, diag):
    inner = extended[1:-1]
    sides = jnp.pad(inner, ((0, 0), (1, 1), (1, 1)))
    beside = extended[2:] + extended[:-2]
    beside = beside + sides[:, 2:, 1:-1] + sides[:, :-2, 1:-1]
    beside = beside + sides[:, 1:-1, 2:] + sides[:, 1:-1, :-2]
    return diag * inner - coupling * beside


def step_whole(rhs, diag_full):
    field = rhs / diag_full
    for weight in sweep_weights(SWEEPS):
        extended = jnp.pad(field, ((1, 1), (0, 0), (0, 0)))
        field = field + weight * (rhs - apply_inner(extended, diag_full)) / diag_full
    return field


def local(state, source, absorption):
    depth_cells = absorption.shape[0]
    offset = lax.axis_index("space") * depth_cells

    def previous(last):
        return shifted(last, "tm", 1)

    stacked = jnp.concatenate([state[:1], source, absorption[None]], axis=0)
    gathered = lax.all_gather(stacked, "space", axis=1, tiled=True)
    source_full = gathered[1 : CF + 1]
    diag_full = 1.0 + 6.0 * coupling + gathered[CF + 1]

    def own_layers(field):
        return lax.dynamic_slice_in_dim(field, offset, depth_cells, 0)

    def back_full(last):
        return lax.all_gather(previous(own_layers(last)), "space", axis=0, tiled=True)

    points = [gathered[0]] + [None] * (CF - 1)

    def relax_full(points):
        for j in range(1, CF):
            points[j] = step_whole(points[j - 1], diag_full) + source_full[j]
        return points

    points = relax_full(points)
    points[0] = step_whole(back_full(points[-1]), diag_full) + source_full[0]
    points = relax_full(points)
    coarse_full = source_full[0] + step_whole(back_full(points[-1]), diag_full) - points[0]
    coarse_residual = own_layers(coarse_full)
    points = [own_layers(point) for point in points]
    residual_norm = lax.psum(jnp.sum(coarse_residual * coarse_residual), ("tm", "space"))
    relaxed = jnp.stack(points, axis=0)
    return (relaxed, coarse_residual[None], residual_norm)


def solution(mesh):
    return jax.shard_map(
        local,
        mesh=mesh,
        in_specs=(
            P("tm", "space", None, None),
            P("tm", "space", None, None),
            P("space", None, None),
        ),
        out_specs=(P("tm", "space", None, None), P("tm", "space", None, None), P()),
        check_vma=False,
    )
```

profile of v0, /device:TPU:0, one launch (start us, length us, event | category | flops | bytes accessed | tf_op | source)
XLA Modules:
  0.0 141.3 jit_solution(12284245266139244024)
XLA Ops:
  7.2 0.9 slice.790
  8.1 2.1 %pad_maximum_fusion = f32[6,4,64,128]{3,2,1,0:T(8,128)} fusion(f32[1,4,64,128]{3,2,1,0:T(8,128)} %bitcast.153, f32[4,4,64,128]{3,2,1,0:T(8,128)} %param.4, f32[1,4,64,128]{3,2,1,0:T(8,128)S(1)} %slice.790), kind=kLoop, calls=%fused_computation.160 | loop fusion | flops 393216 | bytes 1572864 | tf_op jit(solution)/shard_map/concatenate | solution.py:52
  10.2 31.4 %all-gather.2.cloned.1.call-done = f32[6,16,64,128]{3,2,1,0:T(8,128)} async-done(((f32[6,4,64,128]{3,2,1,0:T(8,128)}), f32[6,16,64,128]{3,2,1,0:T(8,128)}) %all-gather.2.cloned.1.call-update) | async-done | bytes 3145744 | tf_op jit(solution)/shard_map/all_gather | solution.py:53
  41.6 1.4 %fusion.424 = f32[16,64,128]{2,1,0:T(8,128)S(1)} fusion(f32[6,16,64,128]{3,2,1,0:T(8,128)} %all-gather.2.cloned.1.call-done), kind=kLoop, calls=%fused_computation.672 | loop fusion | flops 262144 | bytes 1572864 | tf_op jit(solution)/shard_map/div | solution.py:38
  43.1 1.6 %fusion.10 = f32[16,64,128]{2,1,0:T(8,128)S(1)} fusion(f32[16,64,128]{2,1,0:T(8,128)S(1)} %fusion.424, f32[6,16,64,128]{3,2,1,0:T(8,128)} %all-gather.2.cloned.1.call-done), kind=kLoop, calls=%fused_computation.251 | loop fusion | flops 1703936 | bytes 2097152 | tf_op jit(solution)/shard_map/add | solution.py:41
  44.7 0.4 fusion.21
  45.2 0.4 fusion.31
  45.6 0.4 fusion.42
  46.0 0.4 fusion.443
  46.5 0.4 fusion.65
  46.9 0.4 fusion.76
  47.3 0.4 fusion.86
  47.8 0.4 fusion.97
  48.2 0.4 fusion.441
  48.7 0.4 fusion.120
  49.1 0.4 fusion.131
  49.5 0.4 fusion.141
  50.0 0.5 fusion.439
  51.1 3.4 %collective-permute-start = (f32[4,64,128]{2,1,0:T(8,128)S(1)}, f32[4,64,128]{2,1,0:T(8,128)S(1)}, u32[]{:S(2)}, u32[]{:S(2)}) collective-permute-start(f32[4,64,128]{2,1,0:T(8,128)S(1)} %fusion.432), channel_id=1, source_target_pairs={{0,4},{4,8},{8,12},{12,16},{16,20},{20,24},{24,28},{1,5},{5,9},{9,... | collective-permute-start | bytes 393224 | tf_op jit(solution)/shard_map/ppermute | solution.py:18
  54.5 3.1 %collective-permute-done = f32[4,64,128]{2,1,0:T(8,128)S(1)} collective-permute-done((f32[4,64,128]{2,1,0:T(8,128)S(1)}, f32[4,64,128]{2,1,0:T(8,128)S(1)}, u32[]{:S(2)}, u32[]{:S(2)}) %collective-permute-start) | collective-permute-done | bytes 131104 | tf_op jit(solution)/shard_map/ppermute | solution.py:18
  57.6 6.7 %all_gather.10 = f32[16,64,128]{2,1,0:T(8,128)S(1)} all-gather(f32[4,64,128]{2,1,0:T(8,128)S(1)} %collective-permute-done), channel_id=1, replica_groups=mesh['tm'=8,'space'=4] {'space'}, dimensions={0}, use_global_device_ids=true | all-gather | bytes 655360 | tf_op jit(solution)/shard_map/all_gather | solution.py:61
  64.4 0.4 fusion.169
  64.8 0.4 fusion.180
  65.2 0.4 fusion.190
  65.7 0.4 fusion.201
  66.1 0.4 fusion.435
  66.6 0.4 fusion.224
  67.0 0.4 fusion.235
  67.4 0.4 fusion.245
  67.9 0.4 fusion.256
  68.3 0.4 fusion.442
  68.8 0.4 fusion.279
  69.2 0.4 fusion.290
  69.6 0.4 fusion.300
  70.1 0.4 fusion.311
  70.5 0.4 fusion.436
  71.8 0.4 fusion.355
  72.3 0.5 fusion.440
  73.2 4.4 %collective-permute-start.1 = (f32[4,64,128]{2,1,0:T(8,128)S(1)}, f32[4,64,128]{2,1,0:T(8,128)S(1)}, u32[]{:S(2)}, u32[]{:S(2)}) collective-permute-start(f32[4,64,128]{2,1,0:T(8,128)S(1)} %get-tuple-element.24), channel_id=1, source_target_pairs={{0,4},{4,8},{8,12},{12,16},{16,20},{20,24},{24,28},{1,5},{5,9},{9,... | collective-permute-start | bytes 393224 | tf_op jit(solution)/shard_map/ppermute | solution.py:18
  77.6 3.2 %collective-permute-done.1 = f32[4,64,128]{2,1,0:T(8,128)S(1)} collective-permute-done((f32[4,64,128]{2,1,0:T(8,128)S(1)}, f32[4,64,128]{2,1,0:T(8,128)S(1)}, u32[]{:S(2)}, u32[]{:S(2)}) %collective-permute-start.1) | collective-permute-done | bytes 131104 | tf_op jit(solution)/shard_map/ppermute | solution.py:18
  80.8 6.9 %all_gather.11 = f32[16,64,128]{2,1,0:T(8,128)S(1)} all-gather(f32[4,64,128]{2,1,0:T(8,128)S(1)} %collective-permute-done.1), channel_id=1, replica_groups=mesh['tm'=8,'space'=4] {'space'}, dimensions={0}, use_global_device_ids=true | all-gather | bytes 655360 | tf_op jit(solution)/shard_map/all_gather | solution.py:61
  87.8 0.4 fusion.383
  88.3 0.4 fusion.394
  88.7 0.5 fusion.404
  89.2 0.4 fusion.415
  90.0 1.3 multiply_reduce_fusion
  91.3 42.3 %psum.7 = f32[]{:T(128)} all-reduce(f32[]{:T(128)} %get-tuple-element.3), channel_id=1, replica_groups=mesh['tm'=8,'space'=4] {'tm','space'}, use_global_device_ids=true, to_apply=%region_1.2 | all-reduce | flops 1 | bytes 8 | tf_op jit(solution)/shard_map/psum | solution.py:76
  133.6 0.8 pad_maximum_fusion.1
  (15 shorter events, 2.5 us)
Async XLA Ops:
  7.2 34.5 %all-gather.2.cloned.1.call-start = ((), (), s32[]{:S(2)}) async-start(), calls=%async_computation | async-start | bytes 3932160 | tf_op jit(solution)/shard_map/all_gather | solution.py:53
  41.6 3.1 %copy-start = (f32[6,16,64,128]{3,2,1,0:T(8,128)S(1)}, f32[6,16,64,128]{3,2,1,0:T(8,128)}, u32[]{:S(2)}) copy-start(f32[6,16,64,128]{3,2,1,0:T(8,128)} %all-gather.2.cloned.1.call-done) | copy-start | bytes 9437188
  51.1 6.5 %collective-permute-start = (f32[4,64,128]{2,1,0:T(8,128)S(1)}, f32[4,64,128]{2,1,0:T(8,128)S(1)}, u32[]{:S(2)}, u32[]{:S(2)}) collective-permute-start(f32[4,64,128]{2,1,0:T(8,128)S(1)} %fusion.432), channel_id=1, source_target_pairs={{0,4},{4,8},{8,12},{12,16},{16,20},{20,24},{24,28},{1,5},{5,9},{9,... | collective-permute-start | bytes 393224 | tf_op jit(solution)/shard_map/ppermute | solution.py:18
  73.2 7.6 %collective-permute-start.1 = (f32[4,64,128]{2,1,0:T(8,128)S(1)}, f32[4,64,128]{2,1,0:T(8,128)S(1)}, u32[]{:S(2)}, u32[]{:S(2)}) collective-permute-start(f32[4,64,128]{2,1,0:T(8,128)S(1)} %get-tuple-element.24), channel_id=1, source_target_pairs={{0,4},{4,8},{8,12},{12,16},{16,20},{20,24},{24,28},{1,5},{5,9},{9,... | collective-permute-start | bytes 393224 | tf_op jit(solution)/shard_map/ppermute | solution.py:18
Sparse Core Ops, SparseCore 0:
  10.4 31.2 all-gather.1
where the time goes:
time: 142 us; the launch traced here: 141 us
  blocking collectives  55.8 us (39%)
  waiting for transfers between devices  37.7 us (27%)
  other arithmetic  24.6 us (17%)
  between operations  14.3 us (10%)
  starting transfers between devices  7.81 us (6%)
    psum x1, blocking collectives, local(): lax.psum(jnp.sum(coarse_residual * coarse_residual), ('tm', 'space'))  42.3 us
    all_gather x1, waiting for transfers between devices, local(): gathered = lax.all_gather(stacked, 'space', axis=1, tiled=True)  31.4 us
    add x30, other arithmetic, step_whole(): field + weight * (rhs - apply_inner(extended, diag_full)) / diag_full  14.2 us
    all_gather x2, blocking collectives, back_full(): lax.all_gather(previous(own_layers(last)), 'space', axis=0, tiled=True)  13.5 us
    ppermute x2, starting transfers between devices, shifted(): return lax.ppermute(value, axis, pairs)  7.77 us
    ppermute x2, waiting for transfers between devices, shifted(): return lax.ppermute(value, axis, pairs)  6.35 us
    div x8, other arithmetic, step_whole(): field = rhs / diag_full  3.89 us
  transfers between devices with their start and end apart: 3, of which 3 were waited for; matrix products, arithmetic and copies ran while one was open for 0% of the time, Pallas kernels for 0%

commit v1 on v0

v1 whole, which is shorter than its diff:
```python
import functools
import math

import jax
import jax.numpy as jnp
from jax import lax
from jax.experimental import pallas as pl
from jax.experimental.pallas import tpu as pltpu
from jax.sharding import PartitionSpec as P

SWEEPS = 5
COUPLING = 4.0
ROWS = 8


def sweep_weights(count):
    spread = 6.0 * COUPLING / (1.0 + 6.0 * COUPLING)
    return [
        1.0 / (1.0 + spread * math.cos(math.pi * (2 * k + 1) / (2 * count))) for k in range(count)
    ]


def step_polynomial():
    rest = [0.0, 1.0]
    for w in sweep_weights(SWEEPS):
        grown = [0.0] * (len(rest) + 1)
        for i, c in enumerate(rest):
            grown[i] += c * (1.0 - w)
            grown[i + 1] += c * w
        rest = grown
    top = [-c for c in rest]
    top[0] += 1.0
    quotient, carry = [], 0.0
    for c in top[:-1]:
        carry += c
        quotient.append(carry)
    return quotient[0], quotient[2], quotient[4]


def partner(value, axis, bit):
    count = lax.axis_size(axis)
    return lax.ppermute(value, axis, [(i, i ^ bit) for i in range(count)])


def next_slab(value):
    count = lax.axis_size("tm")
    return lax.ppermute(value, "tm", [(i, i + 1) for i in range(count - 1)])


def pieces_of(value):
    count = lax.axis_size("space")
    blocks = [value]
    bit = count // 2
    found = {0: value}
    while bit:
        found.update({m ^ bit: partner(v, "space", bit) for m, v in list(found.items())})
        bit //= 2
    return [found[m] for m in range(count)]


def chain_kernel(count, steps, keep, idx_ref, *refs):
    first = refs[:count]
    rest = refs[count : 2 * count]
    refs = refs[2 * count :]
    if keep:
        before_ref, relaxed_ref, change_ref, norm_ref = refs[:4]
        refs = refs[4:]
    else:
        last_ref, whole_ref = refs[:2]
        refs = refs[2:]
    h_ref, g_ref, a_ref, b_ref, c_ref, d_ref, s_ref, u_ref = refs
    planes, groups, rows, lanes = g_ref.shape
    depth = first[0].shape[-3]
    idx = idx_ref[0]
    c0, c1, c2 = (c / COUPLING for c in step_polynomial())

    def strided(k):
        return pl.ds(k, rows, stride=groups)

    for m in range(count):
        base = (idx ^ m) * depth
        for z in range(depth):
            for k in range(groups):
                diag = 1.0 + 6.0 * COUPLING + rest[m][steps - 1, z, strided(k), :]
                h = COUPLING / diag
                h_ref[base + z, k] = h
                g_ref[base + z, k] = h * first[m][z, strided(k), :]
                for j in range(steps - 1):
                    s_ref[j, base + z, k] = rest[m][j, z, strided(k), :]
                s_ref[steps - 1, base + z, k] = jnp.zeros((rows, lanes), jnp.float32)

    row = lax.broadcasted_iota(jnp.int32, (rows, lanes), 0)
    lane = lax.broadcasted_iota(jnp.int32, (rows, lanes), 1)
    not_top, not_bottom = row != 0, row != rows - 1
    not_left, not_right = lane != 0, lane != lanes - 1

    def jacobi(f_ref, z):
        field = [f_ref[z, k] for k in range(groups)]
        above = jnp.where(not_top, pltpu.roll(field[-1], 1, 0), 0.0)
        below = jnp.where(not_bottom, pltpu.roll(field[0], rows - 1, 0), 0.0)
        for k in range(groups):
            total = (field[k - 1] if k else above) + (field[k + 1] if k < groups - 1 else below)
            if z:
                total = total + f_ref[z - 1, k]
            if z < planes - 1:
                total = total + f_ref[z + 1, k]
            left = jnp.where(not_left, pltpu.roll(field[k], 1, 1), 0.0)
            right = jnp.where(not_right, pltpu.roll(field[k], lanes - 1, 1), 0.0)
            yield k, h_ref[z, k] * (total + (left + right))

    def step(j, carry):
        def level0(z):
            for k, v in jacobi(g_ref, z):
                a_ref[z, k] = v

        def level1(z):
            for k, v in jacobi(a_ref, z):
                b_ref[z, k] = c1 * g_ref[z, k] + c2 * v

        def level2(z):
            for k, v in jacobi(b_ref, z):
                c_ref[z, k] = v

        def level3(z):
            for k, v in jacobi(c_ref, z):
                d_ref[z, k] = c0 * g_ref[z, k] + v

        def level4(z):
            for k, v in jacobi(d_ref, z):
                u = (d_ref[z, k] + v) + s_ref[j, z, k]
                u_ref[j, z, k] = u
                g_ref[z, k] = h_ref[z, k] * u

        levels = [level0, level1, level2, level3, level4]
        for t in range(planes + 2 * (len(levels) - 1)):
            for i, level in enumerate(levels):
                z = t - 2 * i
                if 0 <= z < planes:
                    level(z)
        return carry

    lax.fori_loop(0, steps, step, 0)

    own = idx * depth
    if keep:
        partial = [jnp.zeros((rows, lanes), jnp.float32)] * groups
        for z in range(planes):
            for k in range(groups):
                change = u_ref[steps - 1, z, k] - before_ref[z, k]
                a_ref[z, k] = change
                partial[k] = partial[k] + change * change
        for z in range(depth):
            for k in range(groups):
                at = strided(k)
                relaxed_ref[0, z, at, :] = first[0][z, at, :]
                for j in range(steps - 1):
                    relaxed_ref[j + 1, z, at, :] = u_ref[j, own + z, k]
                change_ref[z, at, :] = a_ref[own + z, k]
        partial = jnp.sum(functools.reduce(jnp.add, partial), axis=0, keepdims=True)
        total = jnp.sum(partial, axis=1, keepdims=True) * idx_ref[1].astype(jnp.float32)
        norm_ref[...] = jnp.broadcast_to(total, norm_ref.shape)
    else:
        for z in range(depth):
            for k in range(groups):
                last_ref[z, strided(k), :] = u_ref[steps - 1, own + z, k]
        for z in range(planes):
            for k in range(groups):
                whole_ref[z, k] = u_ref[steps - 1, z, k]


def chain(idx, first, rest, before=None):
    count = len(first)
    depth, nx, ny = first[0].shape
    steps = rest[0].shape[0]
    planes, groups = depth * count, nx // ROWS
    field = (planes, groups, ROWS, ny)
    quarter = jax.ShapeDtypeStruct((depth, nx, ny), jnp.float32)
    operands = [idx, *first, *rest]
    if before is None:
        outs = (quarter, jax.ShapeDtypeStruct(field, jnp.float32))
    else:
        operands.append(before)
        outs = (
            jax.ShapeDtypeStruct((steps, depth, nx, ny), jnp.float32),
            quarter,
            jax.ShapeDtypeStruct((1, ny), jnp.float32),
        )
    vmem = pl.BlockSpec(memory_space=pltpu.VMEM)
    return pl.pallas_call(
        functools.partial(chain_kernel, count, steps, before is not None),
        out_shape=outs,
        in_specs=[pl.BlockSpec(memory_space=pltpu.SMEM)] + [vmem] * (len(operands) - 1),
        out_specs=jax.tree.map(lambda _: vmem, outs),
        scratch_shapes=[pltpu.VMEM(field, jnp.float32)] * 6 + [pltpu.VMEM((steps, *field), jnp.float32)] * 2,
        name="chain" if before is None else "chain_keep",
    )(*operands)


def local(state, source, absorption):
    space, slab = lax.axis_index("space"), lax.axis_index("tm")
    has_next = (slab < lax.axis_size("tm") - 1).astype(jnp.int32)
    idx = jnp.stack([space.astype(jnp.int32), has_next])
    stacked = jnp.concatenate([source[1:], absorption[None], state[:1]], axis=0)
    gathered = pieces_of(stacked)
    rest = [g[:-1] for g in gathered]
    last, before = chain(idx, [g[-1] for g in gathered], rest)
    coarse = next_slab(last) + source[0]
    relaxed, change, partial = chain(idx, pieces_of(coarse), rest, before)
    residual = next_slab(change)
    bit = 1
    while bit < lax.axis_size("tm"):
        partial = partial + partner(partial, "tm", bit)
        bit *= 2
    return relaxed, residual[None], partial[0, 0]


def solution(mesh):
    return jax.shard_map(
        local,
        mesh=mesh,
        in_specs=(
            P("tm", "space", None, None),
            P("tm", "space", None, None),
            P("space", None, None),
        ),
        out_specs=(P("tm", "space", None, None), P("tm", "space", None, None), P()),
        check_vma=False,
    )
```

time: 142 us -> 78.5 us (0.55)
  blocking collectives: 55.8 us -> 0 us
  other arithmetic: 24.6 us -> 2.92 us
  Pallas kernels: 0 us -> 18.1 us
  between operations: 14.3 us -> 0.72 us
  starting transfers between devices: 7.81 us -> 19.4 us
  waiting for transfers between devices: 37.7 us -> 28.7 us
  local copies, waits for them, and re-layouts: 0.94 us -> 8.48 us
    psum x1 -> x0, blocking collectives: 42.3 us -> none  [local(): lax.psum(jnp.sum(coarse_residual * coarse_residual), ('tm', 'space'))]
    all_gather x1 -> x0, waiting for transfers between devices: 31.4 us -> none  [local(): gathered = lax.all_gather(stacked, 'space', axis=1, tiled=True)]
    ppermute x2 -> x11, waiting for transfers between devices: 6.35 us -> 28.7 us  [the longest x9 25 us: partner(): return lax.ppermute(value, axis, [(i, i ^ bit) for i in range(count)])]
    pallas_call x0 -> x2, Pallas kernels: none -> 18.1 us  [chain(): pl.pallas_call(functools.partial(chain_kernel, count, steps, before is no...]
    all_gather x2 -> x0, blocking collectives: 13.5 us -> none  [back_full(): lax.all_gather(previous(own_layers(last)), 'space', axis=0, tiled=True)]
    add x31 -> x4, other arithmetic: 14.3 us -> 1.44 us  [the longest x1 0.92 us: local(): coarse = next_slab(last) + source[0]]
    ppermute x2 -> x11, starting transfers between devices: 7.77 us -> 19.4 us  [the longest x9 11.3 us: partner(): return lax.ppermute(value, axis, [(i, i ^ bit) for i in range(count)])]
    slice x1 -> x5, local copies, waits for them, and re-layouts: 0.91 us -> 5.18 us  [the longest x2 2.63 us: local(): stacked = jnp.concatenate([source[1:], absorption[None], state[:1]], axis=0)]
  transfers between devices with their start and end apart: 3 -> 11, of which waited for: 3 -> 7; matrix products, arithmetic and copies ran while one was open for 0% -> 6% of each run, Pallas kernels for 0% -> 0%
where the time goes in v1:
time: 78.5 us; the launch traced here: 78.3 us
  waiting for transfers between devices  28.7 us (37%)
  starting transfers between devices  19.4 us (25%)
  Pallas kernels  18.1 us (23%)
  local copies, waits for them, and re-layouts  8.48 us (11%)
  other arithmetic  2.92 us (4%)
    ppermute x9, waiting for transfers between devices, partner(): return lax.ppermute(value, axis, [(i, i ^ bit) for i in range(count)])  25 us
    pallas_call x2, Pallas kernels, chain(): pl.pallas_call(functools.partial(chain_kernel, count, steps, before is no...  18.1 us
    ppermute x9, starting transfers between devices, partner(): return lax.ppermute(value, axis, [(i, i ^ bit) for i in range(count)])  11.3 us
    ppermute x2, starting transfers between devices, next_slab(): return lax.ppermute(value, 'tm', [(i, i + 1) for i in range(count - 1)])  8.02 us
    ppermute x2, waiting for transfers between devices, next_slab(): return lax.ppermute(value, 'tm', [(i, i + 1) for i in range(count - 1)])  3.72 us
    slice x2, local copies, waits for them, and re-layouts, local(): stacked = jnp.concatenate([source[1:], absorption[None], state[:1]], axis=0)  2.63 us
    slice x3, local copies, waits for them, and re-layouts, local(): rest = [g[:-1] for g in gathered]  2.55 us
    squeeze x3, local copies, waits for them, and re-layouts, local(): last, before = chain(idx, [g[-1] for g in gathered], rest)  1.99 us
  transfers between devices with their start and end apart: 11, of which 7 were waited for; matrix products, arithmetic and copies ran while one was open for 6% of the time, Pallas kernels for 0%

profile of v1, /device:TPU:0, one launch (start us, length us, event | category | flops | bytes accessed | tf_op | source)
XLA Modules:
  0.0 78.3 jit_solution(411502581540545008)
XLA Ops:
  0.6 1.6 %fusion = (f32[1,4,64,128]{3,2,1,0:T(8,128)S(1)}, f32[4,64,128]{2,1,0:T(8,128)}) fusion(f32[4,4,64,128]{3,2,1,0:T(8,128)} %param.3), kind=kLoop, calls=%fused_computation.8 | loop fusion | bytes 393216 | tf_op jit(solution)/shard_map/slice | solution.py:203
  2.2 0.0 copy-start
  2.2 1.1 %slice.33 = f32[3,4,64,128]{3,2,1,0:T(8,128)S(1)} slice(f32[4,4,64,128]{3,2,1,0:T(8,128)} %param.4), slice={[1:4], [0:4], [0:64], [0:128]} | slice | bytes 786432 | tf_op jit(solution)/shard_map/slice | solution.py:203
  3.3 0.0 copy-done
  3.3 0.1 pad_maximum_fusion
  3.3 3.1 %collective-permute-start.1 = (f32[5,4,64,128]{3,2,1,0:T(8,128)S(1)}, f32[5,4,64,128]{3,2,1,0:T(8,128)S(1)}, u32[]{:S(2)}, u32[]{:S(2)}) collective-permute-start(f32[5,4,64,128]{3,2,1,0:T(8,128)S(1)} %pad_maximum_fusion), channel_id=1, source_target_pairs={{0,2},{1,3},{2,0},{3,1},{4,6},{5,7},{6,4},{7,5},{8,10},{9,11},{10,... | collective-permute-start | bytes 1966088 | tf_op jit(solution)/shard_map/ppermute | solution.py:42
  6.4 0.0 collective-permute-start
  6.4 14.7 %collective-permute-done.1 = f32[5,4,64,128]{3,2,1,0:T(8,128)S(1)} collective-permute-done((f32[5,4,64,128]{3,2,1,0:T(8,128)S(1)}, f32[5,4,64,128]{3,2,1,0:T(8,128)S(1)}, u32[]{:S(2)}, u32[]{:S(2)}) %collective-permute-start.1) | collective-permute-done | bytes 655392 | tf_op jit(solution)/shard_map/ppermute | solution.py:42
  21.1 0.0 collective-permute-start.2
  21.1 0.6 pad_add_fusion.idx_ref
  21.7 0.8 %pad_maximum_fusion.1.refs_4_ = f32[4,4,64,128]{3,2,1,0:T(8,128)} fusion(f32[1,4,64,128]{3,2,1,0:T(8,128)S(1)} %bitcast.17, f32[3,4,64,128]{3,2,1,0:T(8,128)S(1)} %slice.33), kind=kLoop, calls=%fused_computation.1 | loop fusion | flops 131072 | bytes 1048576 | tf_op jit(solution)/shard_map/concatenate | solution.py:203
  22.6 0.9 %slice.46.refs_6_ = f32[4,4,64,128]{3,2,1,0:T(8,128)} slice(f32[5,4,64,128]{3,2,1,0:T(8,128)S(1)} %collective-permute-done.1), slice={[0:4], [0:4], [0:64], [0:128]} | slice | bytes 1048576 | tf_op jit(solution)/shard_map/slice | solution.py:205
  23.4 0.0 collective-permute-done
  23.4 0.8 %slice.45.refs_5_ = f32[4,4,64,128]{3,2,1,0:T(8,128)} slice(f32[5,4,64,128]{3,2,1,0:T(8,128)S(1)} %collective-permute-done), slice={[0:4], [0:4], [0:64], [0:128]} | slice | bytes 1048576 | tf_op jit(solution)/shard_map/slice | solution.py:205
  24.2 0.7 slice_bitcast_fusion.1.refs_2_
  24.9 0.7 slice_bitcast_fusion.2.refs_1_
  25.6 0.0 collective-permute-done.2
  25.6 0.7 slice_bitcast_fusion.refs_3_
  26.2 0.9 %slice.47.refs_7_ = f32[4,4,64,128]{3,2,1,0:T(8,128)} slice(f32[5,4,64,128]{3,2,1,0:T(8,128)S(1)} %collective-permute-done.2), slice={[0:4], [0:4], [0:64], [0:128]} | slice | bytes 1048576 | tf_op jit(solution)/shard_map/slice | solution.py:205
  27.1 8.9 %chain.1 = (f32[4,64,128]{2,1,0:T(8,128)}, f32[16,8,8,128]{3,2,1,0:T(8,128)}) custom-call(s32[2]{0:T(128)} %pad_add_fusion.idx_ref, f32[4,64,128]{2,1,0:T(8,128)} %get-tuple-element.14.refs_0_, f32[4,64,128]{2,1,0:T(8,128)} %slice_bitcast_fusion.2.refs_1_, f32[4,64,128]{2,1,0:T(8,128)} %slice_bitcast_fusion.1.refs_2_, ...), custom_call_target="tpu_custom_call" | custom-call | tf_op jit(solution)/shard_map/chain/pallas_call | solution.py:189
  36.0 3.6 %collective-permute-start.3 = (f32[4,64,128]{2,1,0:T(8,128)}, f32[4,64,128]{2,1,0:T(8,128)S(1)}, u32[]{:S(2)}, u32[]{:S(2)}) collective-permute-start(f32[4,64,128]{2,1,0:T(8,128)} %get-tuple-element.8), channel_id=1, source_target_pairs={{0,4},{4,8},{8,12},{12,16},{16,20},{20,24},{24,28},{1,5},{5,9},{9,... | collective-permute-start | bytes 393224 | tf_op jit(solution)/shard_map/ppermute | solution.py:47
  39.6 3.7 %collective-permute-done.3 = f32[4,64,128]{2,1,0:T(8,128)S(1)} collective-permute-done((f32[4,64,128]{2,1,0:T(8,128)}, f32[4,64,128]{2,1,0:T(8,128)S(1)}, u32[]{:S(2)}, u32[]{:S(2)}) %collective-permute-start.3) | collective-permute-done | bytes 131104 | tf_op jit(solution)/shard_map/ppermute | solution.py:47
  43.3 0.9 %bitcast_add_fusion.refs_0_ = f32[4,64,128]{2,1,0:T(8,128)S(1)} fusion(f32[4,64,128]{2,1,0:T(8,128)S(1)} %collective-permute-done.3, f32[4,4,64,128]{3,2,1,0:T(8,128)} %param.4), kind=kLoop, calls=%fused_computation.5 | loop fusion | flops 32768 | bytes 393216 | tf_op jit(solution)/shard_map/add | solution.py:207
  44.3 0.0 copy-start.1
  44.3 1.6 %collective-permute-start.5 = (f32[4,64,128]{2,1,0:T(8,128)S(1)}, f32[4,64,128]{2,1,0:T(8,128)S(1)}, u32[]{:S(2)}, u32[]{:S(2)}) collective-permute-start(f32[4,64,128]{2,1,0:T(8,128)S(1)} %bitcast_add_fusion.refs_0_), channel_id=1, source_target_pairs={{0,2},{1,3},{2,0},{3,1},{4,6},{5,7},{6,4},{7,5},{8,10},{9,11},{10,... | collective-permute-start | bytes 393224 | tf_op jit(solution)/shard_map/ppermute | solution.py:42
  45.9 0.0 collective-permute-start.4
  45.9 3.5 %collective-permute-done.5.refs_2_ = f32[4,64,128]{2,1,0:T(8,128)S(1)} collective-permute-done((f32[4,64,128]{2,1,0:T(8,128)S(1)}, f32[4,64,128]{2,1,0:T(8,128)S(1)}, u32[]{:S(2)}, u32[]{:S(2)}) %collective-permute-start.5) | collective-permute-done | bytes 131104 | tf_op jit(solution)/shard_map/ppermute | solution.py:42
  49.4 0.0 collective-permute-start.6
  49.4 0.0 collective-permute-done.4.refs_1_
  49.4 0.0 copy-start.3
  49.4 1.3 %collective-permute-done.6.refs_3_ = f32[4,64,128]{2,1,0:T(8,128)S(1)} collective-permute-done((f32[4,64,128]{2,1,0:T(8,128)S(1)}, f32[4,64,128]{2,1,0:T(8,128)S(1)}, u32[]{:S(2)}, u32[]{:S(2)}) %collective-permute-start.6) | collective-permute-done | bytes 131104 | tf_op jit(solution)/shard_map/ppermute | solution.py:42
  50.7 0.0 copy-start.4
  50.8 0.0 copy-done.1
  50.8 0.0 copy-done.2
  50.8 0.0 copy-done.3
  50.8 0.6 copy-done.4
  51.4 9.2 %chain_keep.1 = (f32[4,4,64,128]{3,2,1,0:T(8,128)}, f32[4,64,128]{2,1,0:T(8,128)}, f32[1,128]{1,0:T(1,128)}) custom-call(s32[2]{0:T(128)} %pad_add_fusion.idx_ref, f32[4,64,128]{2,1,0:T(8,128)} %copy-done.1, f32[4,64,128]{2,1,0:T(8,128)} %copy-done.3, f32[4,64,128]{2,1,0:T(8,128)} %copy-done.2, f32[4,64,128]{2,1,0:T(8,128)} %copy-done.4, ...), custom_call_target="tpu_custom_call" | custom-call | tf_op jit(solution)/shard_map/chain_keep/pallas_call | solution.py:189
  60.6 4.4 %collective-permute-start.7 = (f32[4,64,128]{2,1,0:T(8,128)}, f32[4,64,128]{2,1,0:T(8,128)S(1)}, u32[]{:S(2)}, u32[]{:S(2)}) collective-permute-start(f32[4,64,128]{2,1,0:T(8,128)} %get-tuple-element.11), channel_id=1, source_target_pairs={{0,4},{4,8},{8,12},{12,16},{16,20},{20,24},{24,28},{1,5},{5,9},{9,... | collective-permute-start | bytes 393224 | tf_op jit(solution)/shard_map/ppermute | solution.py:47
  65.0 0.0 copy-done.5
  65.0 2.5 %collective-permute-start.8 = (f32[1,128]{1,0:T(1,128)S(1)}, f32[1,128]{1,0:T(1,128)S(1)}, u32[]{:S(2)}, u32[]{:S(2)}) collective-permute-start(f32[1,128]{1,0:T(1,128)S(1)} %copy-done.5), channel_id=1, source_target_pairs={{0,4},{4,0},{8,12},{12,8},{16,20},{20,16},{24,28},{28,24},{1,5},{5... | collective-permute-start | bytes 1544 | tf_op jit(solution)/shard_map/ppermute | solution.py:42
  67.5 1.5 %collective-permute-done.8 = f32[1,128]{1,0:T(1,128)S(1)} collective-permute-done((f32[1,128]{1,0:T(1,128)S(1)}, f32[1,128]{1,0:T(1,128)S(1)}, u32[]{:S(2)}, u32[]{:S(2)}) %collective-permute-start.8) | collective-permute-done | bytes 544 | tf_op jit(solution)/shard_map/ppermute | solution.py:42
  69.1 1.6 %collective-permute-start.9 = (f32[1,128]{1,0:T(1,128)S(1)}, f32[1,128]{1,0:T(1,128)S(1)}, u32[]{:S(2)}, u32[]{:S(2)}) collective-permute-start(f32[1,128]{1,0:T(1,128)S(1)} %add.13), channel_id=1, source_target_pairs={{0,8},{4,12},{8,0},{12,4},{16,24},{20,28},{24,16},{28,20},{1,9},{5... | collective-permute-start | bytes 1544 | tf_op jit(solution)/shard_map/ppermute | solution.py:42
  70.6 2.0 %collective-permute-done.9 = f32[1,128]{1,0:T(1,128)S(1)} collective-permute-done((f32[1,128]{1,0:T(1,128)S(1)}, f32[1,128]{1,0:T(1,128)S(1)}, u32[]{:S(2)}, u32[]{:S(2)}) %collective-permute-start.9) | collective-permute-done | bytes 544 | tf_op jit(solution)/shard_map/ppermute | solution.py:42
  72.6 2.6 %collective-permute-start.10 = (f32[1,128]{1,0:T(1,128)S(1)}, f32[1,128]{1,0:T(1,128)S(1)}, u32[]{:S(2)}, u32[]{:S(2)}) collective-permute-start(f32[1,128]{1,0:T(1,128)S(1)} %add.14), channel_id=1, source_target_pairs={{0,16},{4,20},{8,24},{12,28},{16,0},{20,4},{24,8},{28,12},{1,17},{... | collective-permute-start | bytes 1544 | tf_op jit(solution)/shard_map/ppermute | solution.py:42
  75.2 1.9 %collective-permute-done.10 = f32[1,128]{1,0:T(1,128)S(1)} collective-permute-done((f32[1,128]{1,0:T(1,128)S(1)}, f32[1,128]{1,0:T(1,128)S(1)}, u32[]{:S(2)}, u32[]{:S(2)}) %collective-permute-start.10) | collective-permute-done | bytes 544 | tf_op jit(solution)/shard_map/ppermute | solution.py:42
  77.1 0.5 add.15
  77.6 0.0 collective-permute-done.7
  77.6 0.7 copy.7
  (4 shorter events, 0.0 us)
Async XLA Ops:
  2.2 1.1 %copy-start = (f32[4,64,128]{2,1,0:T(8,128)S(1)}, f32[4,64,128]{2,1,0:T(8,128)}, u32[]{:S(2)}) copy-start(f32[4,64,128]{2,1,0:T(8,128)} %param.5) | copy-start | bytes 393220
  3.3 17.8 %collective-permute-start.1 = (f32[5,4,64,128]{3,2,1,0:T(8,128)S(1)}, f32[5,4,64,128]{3,2,1,0:T(8,128)S(1)}, u32[]{:S(2)}, u32[]{:S(2)}) collective-permute-start(f32[5,4,64,128]{3,2,1,0:T(8,128)S(1)} %pad_maximum_fusion), channel_id=1, source_target_pairs={{0,2},{1,3},{2,0},{3,1},{4,6},{5,7},{6,4},{7,5},{8,10},{9,11},{10,... | collective-permute-start | bytes 1966088 | tf_op jit(solution)/shard_map/ppermute | solution.py:42
  6.4 17.0 %collective-permute-start = (f32[5,4,64,128]{3,2,1,0:T(8,128)S(1)}, f32[5,4,64,128]{3,2,1,0:T(8,128)S(1)}, u32[]{:S(2)}, u32[]{:S(2)}) collective-permute-start(f32[5,4,64,128]{3,2,1,0:T(8,128)S(1)} %pad_maximum_fusion), channel_id=1, source_target_pairs={{0,1},{1,0},{2,3},{3,2},{4,5},{5,4},{6,7},{7,6},{8,9},{9,8},{10,11... | collective-permute-start | bytes 1966088 | tf_op jit(solution)/shard_map/ppermute | solution.py:42
  21.1 4.4 %collective-permute-start.2 = (f32[5,4,64,128]{3,2,1,0:T(8,128)S(1)}, f32[5,4,64,128]{3,2,1,0:T(8,128)S(1)}, u32[]{:S(2)}, u32[]{:S(2)}) collective-permute-start(f32[5,4,64,128]{3,2,1,0:T(8,128)S(1)} %collective-permute-done.1), channel_id=1, source_target_pairs={{0,1},{1,0},{2,3},{3,2},{4,5},{5,4},{6,7},{7,6},{8,9},{9,8},{10,11... | collective-permute-start | bytes 1966088 | tf_op jit(solution)/shard_map/ppermute | solution.py:42
  36.0 7.3 %collective-permute-start.3 = (f32[4,64,128]{2,1,0:T(8,128)}, f32[4,64,128]{2,1,0:T(8,128)S(1)}, u32[]{:S(2)}, u32[]{:S(2)}) collective-permute-start(f32[4,64,128]{2,1,0:T(8,128)} %get-tuple-element.8), channel_id=1, source_target_pairs={{0,4},{4,8},{8,12},{12,16},{16,20},{20,24},{24,28},{1,5},{5,9},{9,... | collective-permute-start | bytes 393224 | tf_op jit(solution)/shard_map/ppermute | solution.py:47
  44.3 6.5 %copy-start.1 = (f32[4,64,128]{2,1,0:T(8,128)}, f32[4,64,128]{2,1,0:T(8,128)S(1)}, u32[]{:S(2)}) copy-start(f32[4,64,128]{2,1,0:T(8,128)S(1)} %bitcast_add_fusion.refs_0_) | copy-start | bytes 393220
  44.3 5.1 %collective-permute-start.5 = (f32[4,64,128]{2,1,0:T(8,128)S(1)}, f32[4,64,128]{2,1,0:T(8,128)S(1)}, u32[]{:S(2)}, u32[]{:S(2)}) collective-permute-start(f32[4,64,128]{2,1,0:T(8,128)S(1)} %bitcast_add_fusion.refs_0_), channel_id=1, source_target_pairs={{0,2},{1,3},{2,0},{3,1},{4,6},{5,7},{6,4},{7,5},{8,10},{9,11},{10,... | collective-permute-start | bytes 393224 | tf_op jit(solution)/shard_map/ppermute | solution.py:42
  45.9 3.5 %collective-permute-start.4 = (f32[4,64,128]{2,1,0:T(8,128)S(1)}, f32[4,64,128]{2,1,0:T(8,128)S(1)}, u32[]{:S(2)}, u32[]{:S(2)}) collective-permute-start(f32[4,64,128]{2,1,0:T(8,128)S(1)} %bitcast_add_fusion.refs_0_), channel_id=1, source_target_pairs={{0,1},{1,0},{2,3},{3,2},{4,5},{5,4},{6,7},{7,6},{8,9},{9,8},{10,11... | collective-permute-start | bytes 393224 | tf_op jit(solution)/shard_map/ppermute | solution.py:42
  49.4 1.4 %copy-start.2 = (f32[4,64,128]{2,1,0:T(8,128)}, f32[4,64,128]{2,1,0:T(8,128)S(1)}, u32[]{:S(2)}) copy-start(f32[4,64,128]{2,1,0:T(8,128)S(1)} %collective-permute-done.5.refs_2_) | copy-start | bytes 393220
  49.4 1.3 %collective-permute-start.6 = (f32[4,64,128]{2,1,0:T(8,128)S(1)}, f32[4,64,128]{2,1,0:T(8,128)S(1)}, u32[]{:S(2)}, u32[]{:S(2)}) collective-permute-start(f32[4,64,128]{2,1,0:T(8,128)S(1)} %collective-permute-done.5.refs_2_), channel_id=1, source_target_pairs={{0,1},{1,0},{2,3},{3,2},{4,5},{5,4},{6,7},{7,6},{8,9},{9,8},{10,11... | collective-permute-start | bytes 393224 | tf_op jit(solution)/shard_map/ppermute | solution.py:42
  49.4 1.3 %copy-start.3 = (f32[4,64,128]{2,1,0:T(8,128)}, f32[4,64,128]{2,1,0:T(8,128)S(1)}, u32[]{:S(2)}) copy-start(f32[4,64,128]{2,1,0:T(8,128)S(1)} %collective-permute-done.4.refs_1_) | copy-start | bytes 393220
  50.7 0.6 copy-start.4
  60.6 4.4 %copy-start.5 = (f32[1,128]{1,0:T(1,128)S(1)}, f32[1,128]{1,0:T(1,128)}, u32[]{:S(2)}) copy-start(f32[1,128]{1,0:T(1,128)} %get-tuple-element.12) | copy-start | bytes 1540
  60.6 17.0 %collective-permute-start.7 = (f32[4,64,128]{2,1,0:T(8,128)}, f32[4,64,128]{2,1,0:T(8,128)S(1)}, u32[]{:S(2)}, u32[]{:S(2)}) collective-permute-start(f32[4,64,128]{2,1,0:T(8,128)} %get-tuple-element.11), channel_id=1, source_target_pairs={{0,4},{4,8},{8,12},{12,16},{16,20},{20,24},{24,28},{1,5},{5,9},{9,... | collective-permute-start | bytes 393224 | tf_op jit(solution)/shard_map/ppermute | solution.py:47
  65.0 4.1 %collective-permute-start.8 = (f32[1,128]{1,0:T(1,128)S(1)}, f32[1,128]{1,0:T(1,128)S(1)}, u32[]{:S(2)}, u32[]{:S(2)}) collective-permute-start(f32[1,128]{1,0:T(1,128)S(1)} %copy-done.5), channel_id=1, source_target_pairs={{0,4},{4,0},{8,12},{12,8},{16,20},{20,16},{24,28},{28,24},{1,5},{5... | collective-permute-start | bytes 1544 | tf_op jit(solution)/shard_map/ppermute | solution.py:42
  69.1 3.6 %collective-permute-start.9 = (f32[1,128]{1,0:T(1,128)S(1)}, f32[1,128]{1,0:T(1,128)S(1)}, u32[]{:S(2)}, u32[]{:S(2)}) collective-permute-start(f32[1,128]{1,0:T(1,128)S(1)} %add.13), channel_id=1, source_target_pairs={{0,8},{4,12},{8,0},{12,4},{16,24},{20,28},{24,16},{28,20},{1,9},{5... | collective-permute-start | bytes 1544 | tf_op jit(solution)/shard_map/ppermute | solution.py:42
  72.6 4.5 %collective-permute-start.10 = (f32[1,128]{1,0:T(1,128)S(1)}, f32[1,128]{1,0:T(1,128)S(1)}, u32[]{:S(2)}, u32[]{:S(2)}) collective-permute-start(f32[1,128]{1,0:T(1,128)S(1)} %add.14), channel_id=1, source_target_pairs={{0,16},{4,20},{8,24},{12,28},{16,0},{20,4},{24,8},{28,12},{1,17},{... | collective-permute-start | bytes 1544 | tf_op jit(solution)/shard_map/ppermute | solution.py:42

commit v2 on v1

v2 whole, which is shorter than its diff:
```python
import functools
import math

import jax
import jax.numpy as jnp
from jax import lax
from jax.experimental import pallas as pl
from jax.experimental.pallas import tpu as pltpu
from jax.sharding import PartitionSpec as P

SWEEPS = 5
COUPLING = 4.0
ROWS = 8
LAG = 1
VMEM_BYTES = 20 * 1024 * 1024


def sweep_weights(count):
    spread = 6.0 * COUPLING / (1.0 + 6.0 * COUPLING)
    return [
        1.0 / (1.0 + spread * math.cos(math.pi * (2 * k + 1) / (2 * count))) for k in range(count)
    ]


def step_polynomial():
    rest = [0.0, 1.0]
    for w in sweep_weights(SWEEPS):
        grown = [0.0] * (len(rest) + 1)
        for i, c in enumerate(rest):
            grown[i] += c * (1.0 - w)
            grown[i + 1] += c * w
        rest = grown
    top = [-c for c in rest]
    top[0] += 1.0
    quotient, carry = [], 0.0
    for c in top[:-1]:
        carry += c
        quotient.append(carry)
    return quotient[0], quotient[2], quotient[4]


def partner(value, axis, bit):
    count = lax.axis_size(axis)
    return lax.ppermute(value, axis, [(i, i ^ bit) for i in range(count)])


def next_slab(value):
    count = lax.axis_size("tm")
    return lax.ppermute(value, "tm", [(i, i + 1) for i in range(count - 1)])


def across(value):
    return partner(value, "space", lax.axis_size("space") // 2)


def pieces_of(value, crossed):
    count = lax.axis_size("space")
    found = {0: value, count // 2: crossed}
    bit = count // 4
    while bit:
        found.update({m ^ bit: partner(v, "space", bit) for m, v in list(found.items())})
        bit //= 2
    return [found[m] for m in range(count)]


def relax(steps, h_ref, g_ref, a_ref, b_ref, c_ref, d_ref, s_ref, write):
    planes, groups, rows, lanes = g_ref.shape
    c0, c1, c2 = (c / COUPLING for c in step_polynomial())
    row = lax.broadcasted_iota(jnp.int32, (rows, lanes), 0)
    lane = lax.broadcasted_iota(jnp.int32, (rows, lanes), 1)
    not_top, not_bottom = row != 0, row != rows - 1
    not_left, not_right = lane != 0, lane != lanes - 1

    def jacobi(f_ref, z):
        field = [f_ref[z, k] for k in range(groups)]
        above = jnp.where(not_top, pltpu.roll(field[-1], 1, 0), 0.0)
        below = jnp.where(not_bottom, pltpu.roll(field[0], rows - 1, 0), 0.0)
        for k in range(groups):
            total = (field[k - 1] if k else above) + (field[k + 1] if k < groups - 1 else below)
            if z:
                total = total + f_ref[z - 1, k]
            if z < planes - 1:
                total = total + f_ref[z + 1, k]
            left = jnp.where(not_left, pltpu.roll(field[k], 1, 1), 0.0)
            right = jnp.where(not_right, pltpu.roll(field[k], lanes - 1, 1), 0.0)
            yield k, h_ref[z, k] * (total + (left + right))

    def step(j, carry):
        def level0(z):
            for k, v in jacobi(g_ref, z):
                a_ref[z, k] = v

        def level1(z):
            for k, v in jacobi(a_ref, z):
                b_ref[z, k] = c1 * g_ref[z, k] + c2 * v

        def level2(z):
            for k, v in jacobi(b_ref, z):
                c_ref[z, k] = v

        def level3(z):
            for k, v in jacobi(c_ref, z):
                d_ref[z, k] = c0 * g_ref[z, k] + v

        def level4(z):
            for k, v in jacobi(d_ref, z):
                u = (d_ref[z, k] + v) + s_ref[j, z, k]
                write(j, z, k, u)
                g_ref[z, k] = h_ref[z, k] * u

        levels = [level0, level1, level2, level3, level4]
        for t in range(planes + LAG * (len(levels) - 1)):
            for i, level in enumerate(levels):
                z = t - LAG * i
                if 0 <= z < planes:
                    level(z)
        return carry

    lax.fori_loop(0, steps, step, 0)


def strided(k, groups):
    return pl.ds(k, ROWS, stride=groups)


def cells(idx, pieces, groups):
    for m, piece in enumerate(pieces):
        depth = piece.shape[-3]
        for z in range(depth):
            for k in range(groups):
                yield piece, z, strided(k, groups), (idx ^ m) * depth + z, k


def open_kernel(count, idx_ref, *refs):
    pieces, (h_ref, v_ref, g_ref, a_ref, b_ref, c_ref, d_ref, s_ref) = refs[:count], refs[count:]
    groups = g_ref.shape[1]
    zero = jnp.zeros(g_ref.shape[2:], jnp.float32)
    for piece, z, at, plane, k in cells(idx_ref[0], pieces, groups):
        h = COUPLING / (1.0 + 6.0 * COUPLING + piece[1, z, at, :])
        h_ref[plane, k] = h
        g_ref[plane, k] = h * piece[0, z, at, :]
        s_ref[0, plane, k] = piece[2, z, at, :]
        s_ref[1, plane, k] = zero

    def write(j, z, k, u):
        v_ref[z, k] = u

    relax(2, h_ref, g_ref, a_ref, b_ref, c_ref, d_ref, s_ref, write)


def close_kernel(count, idx_ref, h_ref, v_ref, *refs):
    pieces, (whole_ref, half_ref, g_ref, a_ref, b_ref, c_ref, d_ref, s_ref) = refs[:count], refs[count:]
    planes, groups = g_ref.shape[:2]
    steps = s_ref.shape[0]
    zero = jnp.zeros(g_ref.shape[2:], jnp.float32)
    for piece, z, at, plane, k in cells(idx_ref[0], pieces, groups):
        g_ref[plane, k] = h_ref[plane, k] * (v_ref[plane, k] + piece[0, z, at, :])
        for j in range(steps - 1):
            s_ref[j, plane, k] = piece[j + 1, z, at, :]
        s_ref[steps - 1, plane, k] = zero

    def write(j, z, k, u):
        whole_ref[z, k] = u

    relax(steps, h_ref, g_ref, a_ref, b_ref, c_ref, d_ref, s_ref, write)
    start = (idx_ref[0] & 1) * (planes // 2)
    for z in range(planes // 2):
        for k in range(groups):
            half_ref[z, k] = whole_ref[start + z, k]


def final_kernel(count, idx_ref, h_ref, before_ref, mine_ref, other_ref, *refs):
    coarse, opens, closes = refs[:count], refs[count : 2 * count], refs[2 * count : 3 * count]
    relaxed_ref, change_ref, norm_ref, g_ref, a_ref, b_ref, c_ref, d_ref, s_ref, u_ref = refs[3 * count :]
    planes, groups = g_ref.shape[:2]
    steps, depth = relaxed_ref.shape[:2]
    idx = idx_ref[0]
    zero = jnp.zeros(g_ref.shape[2:], jnp.float32)
    start = idx & 1
    for z in range(planes // 2):
        for k in range(groups):
            u_ref[0, start * (planes // 2) + z, k] = mine_ref[z, k]
            u_ref[0, (1 - start) * (planes // 2) + z, k] = other_ref[z, k]
    for piece, z, at, plane, k in cells(idx, coarse, groups):
        u = u_ref[0, plane, k] + piece[0, z, at, :]
        if piece is coarse[0]:
            relaxed_ref[0, z, at, :] = u
        g_ref[plane, k] = h_ref[plane, k] * u
    for piece, z, at, plane, k in cells(idx, opens, groups):
        s_ref[0, plane, k] = piece[2, z, at, :]
        s_ref[steps - 1, plane, k] = zero
    for piece, z, at, plane, k in cells(idx, closes, groups):
        for j in range(1, steps - 1):
            s_ref[j, plane, k] = piece[j - 1, z, at, :]

    def write(j, z, k, u):
        u_ref[j, z, k] = u

    relax(steps, h_ref, g_ref, a_ref, b_ref, c_ref, d_ref, s_ref, write)

    own = idx * depth
    partial = [zero] * groups
    for z in range(planes):
        for k in range(groups):
            change = u_ref[steps - 1, z, k] - before_ref[z, k]
            a_ref[z, k] = change
            partial[k] = partial[k] + change * change
    for z in range(depth):
        for k in range(groups):
            at = strided(k, groups)
            for j in range(steps - 1):
                relaxed_ref[j + 1, z, at, :] = u_ref[j, own + z, k]
            change_ref[z, at, :] = a_ref[own + z, k]
    partial = jnp.sum(functools.reduce(jnp.add, partial), axis=0, keepdims=True)
    total = jnp.sum(partial, axis=1, keepdims=True) * idx_ref[1].astype(jnp.float32)
    norm_ref[...] = jnp.broadcast_to(total, norm_ref.shape)


def call(kernel, name, operands, outs, scratch):
    vmem = pl.BlockSpec(memory_space=pltpu.VMEM)
    return pl.pallas_call(
        kernel,
        out_shape=tuple(jax.ShapeDtypeStruct(shape, jnp.float32) for shape in outs),
        in_specs=[pl.BlockSpec(memory_space=pltpu.SMEM)] + [vmem] * (len(operands) - 1),
        out_specs=(vmem,) * len(outs),
        scratch_shapes=[pltpu.VMEM(shape, jnp.float32) for shape in scratch],
        compiler_params=pltpu.CompilerParams(vmem_limit_bytes=VMEM_BYTES),
        name=name,
    )(*operands)


def local(state, source, absorption):
    space, slab = lax.axis_index("space"), lax.axis_index("tm")
    count, slabs = lax.axis_size("space"), lax.axis_size("tm")
    steps, depth, nx, ny = source.shape
    planes, groups = depth * count, nx // ROWS
    field = (planes, groups, ROWS, ny)
    half = (planes // 2, groups, ROWS, ny)
    has_next = (slab < slabs - 1).astype(jnp.int32)
    idx = jnp.stack([space.astype(jnp.int32), has_next])

    opens = jnp.concatenate([state[:1], absorption[None], source[1:2]], axis=0)
    closes, coarse = source[2:], source[:1]
    crossed = across(opens)
    closes_crossed = across(closes)
    coarse_crossed = across(coarse)
    opens = pieces_of(opens, crossed)

    h, v = call(
        functools.partial(open_kernel, count), "open", [idx, *opens], [field] * 2, [field] * 5 + [(2, *field)]
    )
    closes_crossed, v = lax.optimization_barrier((closes_crossed, v))
    closes = pieces_of(closes, closes_crossed)
    before, mine = call(
        functools.partial(close_kernel, count),
        "close",
        [idx, h, v, *closes],
        [field, half],
        [field] * 5 + [(steps - 2, *field)],
    )
    coarse_crossed, mine = lax.optimization_barrier((coarse_crossed, mine))
    mine = next_slab(mine)
    coarse = pieces_of(coarse, coarse_crossed)
    other = partner(mine, "space", 1)
    relaxed, change, partial = call(
        functools.partial(final_kernel, count),
        "final",
        [idx, h, before, mine, other, *coarse, *opens, *closes],
        [source.shape, (depth, nx, ny), (1, ny)],
        [field] * 5 + [(steps, *field)] * 2,
    )
    residual = next_slab(change)
    bit = 1
    while bit < slabs:
        partial = partial + partner(partial, "tm", bit)
        bit *= 2
    return relaxed, residual[None], partial[0, 0]


def solution(mesh):
    return jax.shard_map(
        local,
        mesh=mesh,
        in_specs=(
            P("tm", "space", None, None),
            P("tm", "space", None, None),
            P("space", None, None),
        ),
        out_specs=(P("tm", "space", None, None), P("tm", "space", None, None), P()),
        check_vma=False,
    )
```

time: 78.5 us -> 65.9 us (0.84)
  local copies, waits for them, and re-layouts: 8.48 us -> 1.74 us
  waiting for transfers between devices: 28.7 us -> 24.3 us
  starting transfers between devices: 19.4 us -> 22 us
  other arithmetic: 2.92 us -> 0.62 us
  Pallas kernels: 18.1 us -> 16.3 us
    ppermute x9 -> x13, waiting for transfers between devices: 25 us -> 18.8 us  [partner(): return lax.ppermute(value, axis, [(i, i ^ bit) for i in range(count)])]
    slice x5 -> x4, local copies, waits for them, and re-layouts: 5.18 us -> 1.05 us  [the longest x2 1.05 us: local(): closes, coarse = (source[2:], source[:1])]
    ppermute x9 -> x13, starting transfers between devices: 11.3 us -> 14 us  [partner(): return lax.ppermute(value, axis, [(i, i ^ bit) for i in range(count)])]
    squeeze x3 -> x0, local copies, waits for them, and re-layouts: 1.99 us -> none  [local(): last, before = chain(idx, [g[-1] for g in gathered], rest)]
    ppermute x2, waiting for transfers between devices: 3.72 us -> 5.54 us  [next_slab(): return lax.ppermute(value, 'tm', [(i, i + 1) for i in range(count - 1)])]
    pallas_call x2 -> x3, Pallas kernels: 18.1 us -> 16.3 us  [call(): pl.pallas_call(kernel, out_shape=tuple((jax.ShapeDtypeStruct(shape, jnp.f...]
    add x1 -> x0, other arithmetic: 0.92 us -> none  [local(): coarse = next_slab(last) + source[0]]
    concatenate x2 -> x1, other arithmetic: 0.89 us -> 0.03 us  [local(): opens = jnp.concatenate([state[:1], absorption[None], source[1:2]], axis=0)]
  transfers between devices with their start and end apart: 11 -> 15, of which waited for: 7 -> 9; matrix products, arithmetic and copies ran while one was open for 6% -> 1% of each run, Pallas kernels for 0% -> 12%
where the time goes in v2:
time: 65.9 us; the launch traced here: 65.7 us
  waiting for transfers between devices  24.3 us (37%)
  starting transfers between devices  22 us (33%)
  Pallas kernels  16.3 us (25%)
  local copies, waits for them, and re-layouts  1.74 us (3%)
  between operations  0.72 us (1%)
    ppermute x13, waiting for transfers between devices, partner(): return lax.ppermute(value, axis, [(i, i ^ bit) for i in range(count)])  18.8 us
    pallas_call x3, Pallas kernels, call(): pl.pallas_call(kernel, out_shape=tuple((jax.ShapeDtypeStruct(shape, jnp.f...  16.3 us
    ppermute x13, starting transfers between devices, partner(): return lax.ppermute(value, axis, [(i, i ^ bit) for i in range(count)])  14 us
    ppermute x2, starting transfers between devices, next_slab(): return lax.ppermute(value, 'tm', [(i, i + 1) for i in range(count - 1)])  8 us
    ppermute x2, waiting for transfers between devices, next_slab(): return lax.ppermute(value, 'tm', [(i, i + 1) for i in range(count - 1)])  5.54 us
  transfers between devices with their start and end apart: 15, of which 9 were waited for; matrix products, arithmetic and copies ran while one was open for 1% of the time, Pallas kernels for 12%

profile of v2, /device:TPU:0, one launch (start us, length us, event | category | flops | bytes accessed | tf_op | source)
XLA Modules:
  0.0 65.7 jit_solution(391358832141537510)
XLA Ops:
  0.6 0.0 slice-start
  0.6 0.0 copy-start.1
  0.7 1.0 %fusion = (f32[1,4,64,128]{3,2,1,0:T(8,128)S(1)}, f32[1,4,64,128]{3,2,1,0:T(8,128)S(1)}) fusion(f32[4,4,64,128]{3,2,1,0:T(8,128)} %param.4), kind=kLoop, calls=%fused_computation.2 | loop fusion | bytes 524288 | tf_op jit(solution)/shard_map/slice | solution.py:243
  1.7 0.0 copy-start
  1.7 0.0 slice-done
  1.7 0.0 copy-done.1
  1.8 3.1 %collective-permute-start.1 = (f32[3,4,64,128]{3,2,1,0:T(8,128)S(1)}, f32[3,4,64,128]{3,2,1,0:T(8,128)S(1)}, u32[]{:S(2)}, u32[]{:S(2)}) collective-permute-start(f32[3,4,64,128]{3,2,1,0:T(8,128)S(1)} %pad_maximum_fusion.refs_0_.refs_4_), channel_id=1, source_target_pairs={{0,2},{1,3},{2,0},{3,1},{4,6},{5,7},{6,4},{7,5},{8,10},{9,11},{10,... | collective-permute-start | bytes 1179656 | tf_op jit(solution)/shard_map/ppermute | solution.py:44
  4.8 0.0 collective-permute-start
  4.8 9.1 %collective-permute-done.1.refs_2_.refs_6_ = f32[3,4,64,128]{3,2,1,0:T(8,128)S(1)} collective-permute-done((f32[3,4,64,128]{3,2,1,0:T(8,128)S(1)}, f32[3,4,64,128]{3,2,1,0:T(8,128)S(1)}, u32[]{:S(2)}, u32[]{:S(2)}) %collective-permute-start.1) | collective-permute-done | bytes 393248 | tf_op jit(solution)/shard_map/ppermute | solution.py:44
  13.9 0.0 collective-permute-start.2
  13.9 0.0 copy-done
  14.0 1.8 %collective-permute-start.3 = (f32[2,4,64,128]{3,2,1,0:T(8,128)S(1)}, f32[2,4,64,128]{3,2,1,0:T(8,128)S(1)}, u32[]{:S(2)}, u32[]{:S(2)}) collective-permute-start(f32[2,4,64,128]{3,2,1,0:T(8,128)S(1)} %slice.17.refs_0_.refs_8_), channel_id=1, source_target_pairs={{0,2},{1,3},{2,0},{3,1},{4,6},{5,7},{6,4},{7,5},{8,10},{9,11},{10,... | collective-permute-start | bytes 786440 | tf_op jit(solution)/shard_map/ppermute | solution.py:44
  15.8 0.2 collective-permute-start.4
  16.0 0.1 pad_add_fusion.idx_ref
  16.1 0.0 collective-permute-done.refs_1_.refs_5_
  16.1 0.0 collective-permute-done.2.refs_3_.refs_7_
  16.1 4.0 %open.1 = (f32[16,8,8,128]{3,2,1,0:T(8,128)S(1)}, f32[16,8,8,128]{3,2,1,0:T(8,128)S(1)}) custom-call(s32[2]{0:T(128)S(1)} %pad_add_fusion.idx_ref, f32[3,4,64,128]{3,2,1,0:T(8,128)S(1)} %pad_maximum_fusion.refs_0_.refs_4_, f32[3,4,64,128]{3,2,1,0:T(8,128)S(1)} %collective-permute-done.refs_1_.refs_5_, ...), custom_call_target="tpu_custom_call" | custom-call | tf_op jit(solution)/shard_map/open/pallas_call | solution.py:221
  20.1 2.7 %collective-permute-done.3.refs_2_.refs_10_ = f32[2,4,64,128]{3,2,1,0:T(8,128)S(1)} collective-permute-done((f32[2,4,64,128]{3,2,1,0:T(8,128)S(1)}, f32[2,4,64,128]{3,2,1,0:T(8,128)S(1)}, u32[]{:S(2)}, u32[]{:S(2)}) %collective-permute-start.3) | collective-permute-done | bytes 262176 | tf_op jit(solution)/shard_map/ppermute | solution.py:44
  22.7 0.0 collective-permute-start.5
  22.7 1.7 %collective-permute-start.6 = (f32[1,4,64,128]{3,2,1,0:T(8,128)S(1)}, f32[1,4,64,128]{3,2,1,0:T(8,128)S(1)}, u32[]{:S(2)}, u32[]{:S(2)}) collective-permute-start(f32[1,4,64,128]{3,2,1,0:T(8,128)S(1)} %get-tuple-element.25.refs_0_), channel_id=1, source_target_pairs={{0,2},{1,3},{2,0},{3,1},{4,6},{5,7},{6,4},{7,5},{8,10},{9,11},{10,... | collective-permute-start | bytes 393224 | tf_op jit(solution)/shard_map/ppermute | solution.py:44
  24.5 0.0 collective-permute-done.4.refs_1_.refs_9_
  24.5 0.0 collective-permute-done.5.refs_3_.refs_11_
  24.5 4.0 %close.1 = (f32[16,8,8,128]{3,2,1,0:T(8,128)S(1)}, f32[8,8,8,128]{3,2,1,0:T(8,128)S(1)}) custom-call(s32[2]{0:T(128)S(1)} %pad_add_fusion.idx_ref, f32[16,8,8,128]{3,2,1,0:T(8,128)S(1)} %get-tuple-element.14.h_ref, f32[16,8,8,128]{3,2,1,0:T(8,128)S(1)} %get-tuple-element.16.v_ref, f32[2,4,64,128]{3,2,1,0:T(8,128)S(1)} %slice.17.refs_0_.refs_8_, ...), custom_call_target="tpu_custom_call" | custom-call | tf_op jit(solution)/shard_map/close/pallas_call | solution.py:221
  28.5 0.2 collective-permute-done.6.refs_2_
  28.7 3.6 %collective-permute-start.7 = (f32[8,8,8,128]{3,2,1,0:T(8,128)S(1)}, f32[8,8,8,128]{3,2,1,0:T(8,128)S(1)}, u32[]{:S(2)}, u32[]{:S(2)}) collective-permute-start(f32[8,8,8,128]{3,2,1,0:T(8,128)S(1)} %get-tuple-element.20), channel_id=1, source_target_pairs={{0,4},{4,8},{8,12},{12,16},{16,20},{20,24},{24,28},{1,5},{5,9},{9,... | collective-permute-start | bytes 786440 | tf_op jit(solution)/shard_map/ppermute | solution.py:49
  32.3 5.5 %collective-permute-done.7.mine_ref = f32[8,8,8,128]{3,2,1,0:T(8,128)S(1)} collective-permute-done((f32[8,8,8,128]{3,2,1,0:T(8,128)S(1)}, f32[8,8,8,128]{3,2,1,0:T(8,128)S(1)}, u32[]{:S(2)}, u32[]{:S(2)}) %collective-permute-start.7) | collective-permute-done | bytes 262176 | tf_op jit(solution)/shard_map/ppermute | solution.py:49
  37.8 0.0 collective-permute-start.8
  37.8 0.5 collective-permute-start.9
  38.3 0.0 collective-permute-start.10
  38.3 1.2 %collective-permute-done.9.refs_1_ = f32[1,4,64,128]{3,2,1,0:T(8,128)S(1)} collective-permute-done((f32[1,4,64,128]{3,2,1,0:T(8,128)S(1)}, f32[1,4,64,128]{3,2,1,0:T(8,128)S(1)}, u32[]{:S(2)}, u32[]{:S(2)}) %collective-permute-start.9) | collective-permute-done | bytes 131104 | tf_op jit(solution)/shard_map/ppermute | solution.py:44
  39.5 0.2 collective-permute-done.10.refs_3_
  39.7 0.0 collective-permute-done.8.other_ref
  39.7 8.3 %final.1 = (f32[4,4,64,128]{3,2,1,0:T(8,128)}, f32[4,64,128]{2,1,0:T(8,128)S(1)}, f32[1,128]{1,0:T(1,128)S(1)}) custom-call(s32[2]{0:T(128)S(1)} %pad_add_fusion.idx_ref, f32[16,8,8,128]{3,2,1,0:T(8,128)S(1)} %get-tuple-element.14.h_ref, f32[16,8,8,128]{3,2,1,0:T(8,128)S(1)} %get-tuple-element.18.before_ref, ...), custom_call_target="tpu_custom_call" | custom-call | tf_op jit(solution)/shard_map/final/pallas_call | solution.py:221
  48.1 4.4 %collective-permute-start.11 = (f32[4,64,128]{2,1,0:T(8,128)S(1)}, f32[4,64,128]{2,1,0:T(8,128)S(1)}, u32[]{:S(2)}, u32[]{:S(2)}) collective-permute-start(f32[4,64,128]{2,1,0:T(8,128)S(1)} %get-tuple-element.23), channel_id=1, source_target_pairs={{0,4},{4,8},{8,12},{12,16},{16,20},{20,24},{24,28},{1,5},{5,9},{9,... | collective-permute-start | bytes 393224 | tf_op jit(solution)/shard_map/ppermute | solution.py:49
  52.4 2.5 %collective-permute-start.12 = (f32[1,128]{1,0:T(1,128)S(1)}, f32[1,128]{1,0:T(1,128)S(1)}, u32[]{:S(2)}, u32[]{:S(2)}) collective-permute-start(f32[1,128]{1,0:T(1,128)S(1)} %get-tuple-element.24), channel_id=1, source_target_pairs={{0,4},{4,0},{8,12},{12,8},{16,20},{20,16},{24,28},{28,24},{1,5},{5... | collective-permute-start | bytes 1544 | tf_op jit(solution)/shard_map/ppermute | solution.py:44
  55.0 1.5 %collective-permute-done.12 = f32[1,128]{1,0:T(1,128)S(1)} collective-permute-done((f32[1,128]{1,0:T(1,128)S(1)}, f32[1,128]{1,0:T(1,128)S(1)}, u32[]{:S(2)}, u32[]{:S(2)}) %collective-permute-start.12) | collective-permute-done | bytes 544 | tf_op jit(solution)/shard_map/ppermute | solution.py:44
  56.5 1.6 %collective-permute-start.13 = (f32[1,128]{1,0:T(1,128)S(1)}, f32[1,128]{1,0:T(1,128)S(1)}, u32[]{:S(2)}, u32[]{:S(2)}) collective-permute-start(f32[1,128]{1,0:T(1,128)S(1)} %add.9), channel_id=1, source_target_pairs={{0,8},{4,12},{8,0},{12,4},{16,24},{20,28},{24,16},{28,20},{1,9},{5... | collective-permute-start | bytes 1544 | tf_op jit(solution)/shard_map/ppermute | solution.py:44
  58.1 2.0 %collective-permute-done.13 = f32[1,128]{1,0:T(1,128)S(1)} collective-permute-done((f32[1,128]{1,0:T(1,128)S(1)}, f32[1,128]{1,0:T(1,128)S(1)}, u32[]{:S(2)}, u32[]{:S(2)}) %collective-permute-start.13) | collective-permute-done | bytes 544 | tf_op jit(solution)/shard_map/ppermute | solution.py:44
  60.1 2.6 %collective-permute-start.14 = (f32[1,128]{1,0:T(1,128)S(1)}, f32[1,128]{1,0:T(1,128)S(1)}, u32[]{:S(2)}, u32[]{:S(2)}) collective-permute-start(f32[1,128]{1,0:T(1,128)S(1)} %add.10), channel_id=1, source_target_pairs={{0,16},{4,20},{8,24},{12,28},{16,0},{20,4},{24,8},{28,12},{1,17},{... | collective-permute-start | bytes 1544 | tf_op jit(solution)/shard_map/ppermute | solution.py:44
  62.7 1.9 %collective-permute-done.14 = f32[1,128]{1,0:T(1,128)S(1)} collective-permute-done((f32[1,128]{1,0:T(1,128)S(1)}, f32[1,128]{1,0:T(1,128)S(1)}, u32[]{:S(2)}, u32[]{:S(2)}) %collective-permute-start.14) | collective-permute-done | bytes 544 | tf_op jit(solution)/shard_map/ppermute | solution.py:44
  64.5 0.5 add.11
  65.1 0.0 collective-permute-done.11
  65.1 0.7 copy.7
  (4 shorter events, 0.1 us)
Async XLA Ops:
  0.6 1.1 %slice-start = ((f32[4,4,64,128]{3,2,1,0:T(8,128)}), f32[1,4,64,128]{3,2,1,0:T(8,128)S(1)}, s32[]{:S(2)}) async-start(f32[4,4,64,128]{3,2,1,0:T(8,128)} %param.3), calls=%async_computation | async-start | bytes 262144 | tf_op jit(solution)/shard_map/slice | solution.py:242
  0.6 1.1 %copy-start.1 = (f32[4,64,128]{2,1,0:T(8,128)S(1)}, f32[4,64,128]{2,1,0:T(8,128)}, u32[]{:S(2)}) copy-start(f32[4,64,128]{2,1,0:T(8,128)} %param.5) | copy-start | bytes 393220
  1.7 12.3 %copy-start = (f32[4,4,64,128]{3,2,1,0:T(8,128)S(1)}, f32[4,4,64,128]{3,2,1,0:T(8,128)}, u32[]{:S(2)}) copy-start(f32[4,4,64,128]{3,2,1,0:T(8,128)} %param.4) | copy-start | bytes 1572868
  1.8 12.2 %collective-permute-start.1 = (f32[3,4,64,128]{3,2,1,0:T(8,128)S(1)}, f32[3,4,64,128]{3,2,1,0:T(8,128)S(1)}, u32[]{:S(2)}, u32[]{:S(2)}) collective-permute-start(f32[3,4,64,128]{3,2,1,0:T(8,128)S(1)} %pad_maximum_fusion.refs_0_.refs_4_), channel_id=1, source_target_pairs={{0,2},{1,3},{2,0},{3,1},{4,6},{5,7},{6,4},{7,5},{8,10},{9,11},{10,... | collective-permute-start | bytes 1179656 | tf_op jit(solution)/shard_map/ppermute | solution.py:44
  4.8 11.3 %collective-permute-start = (f32[3,4,64,128]{3,2,1,0:T(8,128)S(1)}, f32[3,4,64,128]{3,2,1,0:T(8,128)S(1)}, u32[]{:S(2)}, u32[]{:S(2)}) collective-permute-start(f32[3,4,64,128]{3,2,1,0:T(8,128)S(1)} %pad_maximum_fusion.refs_0_.refs_4_), channel_id=1, source_target_pairs={{0,1},{1,0},{2,3},{3,2},{4,5},{5,4},{6,7},{7,6},{8,9},{9,8},{10,11... | collective-permute-start | bytes 1179656 | tf_op jit(solution)/shard_map/ppermute | solution.py:44
  13.9 2.1 %collective-permute-start.2 = (f32[3,4,64,128]{3,2,1,0:T(8,128)S(1)}, f32[3,4,64,128]{3,2,1,0:T(8,128)S(1)}, u32[]{:S(2)}, u32[]{:S(2)}) collective-permute-start(f32[3,4,64,128]{3,2,1,0:T(8,128)S(1)} %collective-permute-done.1.refs_2_.refs_6_), channel_id=1, source_target_pairs={{0,1},{1,0},{2,3},{3,2},{4,5},{5,4},{6,7},{7,6},{8,9},{9,8},{10,11... | collective-permute-start | bytes 1179656 | tf_op jit(solution)/shard_map/ppermute | solution.py:44
  14.0 8.8 %collective-permute-start.3 = (f32[2,4,64,128]{3,2,1,0:T(8,128)S(1)}, f32[2,4,64,128]{3,2,1,0:T(8,128)S(1)}, u32[]{:S(2)}, u32[]{:S(2)}) collective-permute-start(f32[2,4,64,128]{3,2,1,0:T(8,128)S(1)} %slice.17.refs_0_.refs_8_), channel_id=1, source_target_pairs={{0,2},{1,3},{2,0},{3,1},{4,6},{5,7},{6,4},{7,5},{8,10},{9,11},{10,... | collective-permute-start | bytes 786440 | tf_op jit(solution)/shard_map/ppermute | solution.py:44
  15.8 8.7 %collective-permute-start.4 = (f32[2,4,64,128]{3,2,1,0:T(8,128)S(1)}, f32[2,4,64,128]{3,2,1,0:T(8,128)S(1)}, u32[]{:S(2)}, u32[]{:S(2)}) collective-permute-start(f32[2,4,64,128]{3,2,1,0:T(8,128)S(1)} %slice.17.refs_0_.refs_8_), channel_id=1, source_target_pairs={{0,1},{1,0},{2,3},{3,2},{4,5},{5,4},{6,7},{7,6},{8,9},{9,8},{10,11... | collective-permute-start | bytes 786440 | tf_op jit(solution)/shard_map/ppermute | solution.py:44
  22.7 1.8 %collective-permute-start.5 = (f32[2,4,64,128]{3,2,1,0:T(8,128)S(1)}, f32[2,4,64,128]{3,2,1,0:T(8,128)S(1)}, u32[]{:S(2)}, u32[]{:S(2)}) collective-permute-start(f32[2,4,64,128]{3,2,1,0:T(8,128)S(1)} %collective-permute-done.3.refs_2_.refs_10_), channel_id=1, source_target_pairs={{0,1},{1,0},{2,3},{3,2},{4,5},{5,4},{6,7},{7,6},{8,9},{9,8},{10,11... | collective-permute-start | bytes 786440 | tf_op jit(solution)/shard_map/ppermute | solution.py:44
  22.7 5.9 %collective-permute-start.6 = (f32[1,4,64,128]{3,2,1,0:T(8,128)S(1)}, f32[1,4,64,128]{3,2,1,0:T(8,128)S(1)}, u32[]{:S(2)}, u32[]{:S(2)}) collective-permute-start(f32[1,4,64,128]{3,2,1,0:T(8,128)S(1)} %get-tuple-element.25.refs_0_), channel_id=1, source_target_pairs={{0,2},{1,3},{2,0},{3,1},{4,6},{5,7},{6,4},{7,5},{8,10},{9,11},{10,... | collective-permute-start | bytes 393224 | tf_op jit(solution)/shard_map/ppermute | solution.py:44
  28.7 9.2 %collective-permute-start.7 = (f32[8,8,8,128]{3,2,1,0:T(8,128)S(1)}, f32[8,8,8,128]{3,2,1,0:T(8,128)S(1)}, u32[]{:S(2)}, u32[]{:S(2)}) collective-permute-start(f32[8,8,8,128]{3,2,1,0:T(8,128)S(1)} %get-tuple-element.20), channel_id=1, source_target_pairs={{0,4},{4,8},{8,12},{12,16},{16,20},{20,24},{24,28},{1,5},{5,9},{9,... | collective-permute-start | bytes 786440 | tf_op jit(solution)/shard_map/ppermute | solution.py:49
  37.8 1.9 %collective-permute-start.8 = (f32[8,8,8,128]{3,2,1,0:T(8,128)S(1)}, f32[8,8,8,128]{3,2,1,0:T(8,128)S(1)}, u32[]{:S(2)}, u32[]{:S(2)}) collective-permute-start(f32[8,8,8,128]{3,2,1,0:T(8,128)S(1)} %collective-permute-done.7.mine_ref), channel_id=1, source_target_pairs={{0,1},{1,0},{2,3},{3,2},{4,5},{5,4},{6,7},{7,6},{8,9},{9,8},{10,11... | collective-permute-start | bytes 786440 | tf_op jit(solution)/shard_map/ppermute | solution.py:44
  37.8 1.7 %collective-permute-start.9 = (f32[1,4,64,128]{3,2,1,0:T(8,128)S(1)}, f32[1,4,64,128]{3,2,1,0:T(8,128)S(1)}, u32[]{:S(2)}, u32[]{:S(2)}) collective-permute-start(f32[1,4,64,128]{3,2,1,0:T(8,128)S(1)} %get-tuple-element.25.refs_0_), channel_id=1, source_target_pairs={{0,1},{1,0},{2,3},{3,2},{4,5},{5,4},{6,7},{7,6},{8,9},{9,8},{10,11... | collective-permute-start | bytes 393224 | tf_op jit(solution)/shard_map/ppermute | solution.py:44
  38.3 1.4 %collective-permute-start.10 = (f32[1,4,64,128]{3,2,1,0:T(8,128)S(1)}, f32[1,4,64,128]{3,2,1,0:T(8,128)S(1)}, u32[]{:S(2)}, u32[]{:S(2)}) collective-permute-start(f32[1,4,64,128]{3,2,1,0:T(8,128)S(1)} %collective-permute-done.6.refs_2_), channel_id=1, source_target_pairs={{0,1},{1,0},{2,3},{3,2},{4,5},{5,4},{6,7},{7,6},{8,9},{9,8},{10,11... | collective-permute-start | bytes 393224 | tf_op jit(solution)/shard_map/ppermute | solution.py:44
  48.1 17.0 %collective-permute-start.11 = (f32[4,64,128]{2,1,0:T(8,128)S(1)}, f32[4,64,128]{2,1,0:T(8,128)S(1)}, u32[]{:S(2)}, u32[]{:S(2)}) collective-permute-start(f32[4,64,128]{2,1,0:T(8,128)S(1)} %get-tuple-element.23), channel_id=1, source_target_pairs={{0,4},{4,8},{8,12},{12,16},{16,20},{20,24},{24,28},{1,5},{5,9},{9,... | collective-permute-start | bytes 393224 | tf_op jit(solution)/shard_map/ppermute | solution.py:49
  52.4 4.1 %collective-permute-start.12 = (f32[1,128]{1,0:T(1,128)S(1)}, f32[1,128]{1,0:T(1,128)S(1)}, u32[]{:S(2)}, u32[]{:S(2)}) collective-permute-start(f32[1,128]{1,0:T(1,128)S(1)} %get-tuple-element.24), channel_id=1, source_target_pairs={{0,4},{4,0},{8,12},{12,8},{16,20},{20,16},{24,28},{28,24},{1,5},{5... | collective-permute-start | bytes 1544 | tf_op jit(solution)/shard_map/ppermute | solution.py:44
  56.5 3.6 %collective-permute-start.13 = (f32[1,128]{1,0:T(1,128)S(1)}, f32[1,128]{1,0:T(1,128)S(1)}, u32[]{:S(2)}, u32[]{:S(2)}) collective-permute-start(f32[1,128]{1,0:T(1,128)S(1)} %add.9), channel_id=1, source_target_pairs={{0,8},{4,12},{8,0},{12,4},{16,24},{20,28},{24,16},{28,20},{1,9},{5... | collective-permute-start | bytes 1544 | tf_op jit(solution)/shard_map/ppermute | solution.py:44
  60.1 4.5 %collective-permute-start.14 = (f32[1,128]{1,0:T(1,128)S(1)}, f32[1,128]{1,0:T(1,128)S(1)}, u32[]{:S(2)}, u32[]{:S(2)}) collective-permute-start(f32[1,128]{1,0:T(1,128)S(1)} %add.10), channel_id=1, source_target_pairs={{0,16},{4,20},{8,24},{12,28},{16,0},{20,4},{24,8},{28,12},{1,17},{... | collective-permute-start | bytes 1544 | tf_op jit(solution)/shard_map/ppermute | solution.py:44

commit v3 on v2

--- a/solution.py
+++ b/solution.py
@@ -169,29 +169,38 @@
             half_ref[z, k] = whole_ref[start + z, k]
 
 
-def final_kernel(count, idx_ref, h_ref, before_ref, mine_ref, other_ref, *refs):
+def sort_kernel(count, idx_ref, *refs):
     coarse, opens, closes = refs[:count], refs[count : 2 * count], refs[2 * count : 3 * count]
-    relaxed_ref, change_ref, norm_ref, g_ref, a_ref, b_ref, c_ref, d_ref, s_ref, u_ref = refs[3 * count :]
+    s_ref = refs[3 * count]
+    groups = s_ref.shape[2]
+    steps = s_ref.shape[0] - 1
+    zero = jnp.zeros(s_ref.shape[3:], jnp.float32)
+    for piece, z, at, plane, k in cells(idx_ref[0], coarse, groups):
+        s_ref[steps, plane, k] = piece[0, z, at, :]
+        s_ref[steps - 1, plane, k] = zero
+    for piece, z, at, plane, k in cells(idx_ref[0], opens, groups):
+        s_ref[0, plane, k] = piece[2, z, at, :]
+    for piece, z, at, plane, k in cells(idx_ref[0], closes, groups):
+        for j in range(1, steps - 1):
+            s_ref[j, plane, k] = piece[j - 1, z, at, :]
+
+
+def final_kernel(idx_ref, h_ref, before_ref, s_ref, mine_ref, other_ref, *refs):
+    relaxed_ref, change_ref, norm_ref, g_ref, a_ref, b_ref, c_ref, d_ref, u_ref = refs
     planes, groups = g_ref.shape[:2]
     steps, depth = relaxed_ref.shape[:2]
     idx = idx_ref[0]
     zero = jnp.zeros(g_ref.shape[2:], jnp.float32)
-    start = idx & 1
-    for z in range(planes // 2):
-        for k in range(groups):
-            u_ref[0, start * (planes // 2) + z, k] = mine_ref[z, k]
-            u_ref[0, (1 - start) * (planes // 2) + z, k] = other_ref[z, k]
-    for piece, z, at, plane, k in cells(idx, coarse, groups):
-        u = u_ref[0, plane, k] + piece[0, z, at, :]
-        if piece is coarse[0]:
-            relaxed_ref[0, z, at, :] = u
-        g_ref[plane, k] = h_ref[plane, k] * u
-    for piece, z, at, plane, k in cells(idx, opens, groups):
-        s_ref[0, plane, k] = piece[2, z, at, :]
-        s_ref[steps - 1, plane, k] = zero
-    for piece, z, at, plane, k in cells(idx, closes, groups):
-        for j in range(1, steps - 1):
-            s_ref[j, plane, k] = piece[j - 1, z, at, :]
+    for part, received in (((idx & 1), mine_ref), (1 - (idx & 1), other_ref)):
+        for z in range(planes // 2):
+            plane = part * (planes // 2) + z
+            for k in range(groups):
+                u = received[z, k] + s_ref[steps, plane, k]
+                a_ref[plane, k] = u
+                g_ref[plane, k] = h_ref[plane, k] * u
+    for z in range(depth):
+        for k in range(groups):
+            relaxed_ref[0, z, strided(k, groups), :] = a_ref[idx * depth + z, k]
 
     def write(j, z, k, u):
         u_ref[j, z, k] = u
@@ -216,7 +225,7 @@
     norm_ref[...] = jnp.broadcast_to(total, norm_ref.shape)
 
 
-def call(kernel, name, operands, outs, scratch):
+def call(kernel, operands, outs, scratch):
     vmem = pl.BlockSpec(memory_space=pltpu.VMEM)
     return pl.pallas_call(
         kernel,
@@ -225,11 +234,10 @@
         out_specs=(vmem,) * len(outs),
         scratch_shapes=[pltpu.VMEM(shape, jnp.float32) for shape in scratch],
         compiler_params=pltpu.CompilerParams(vmem_limit_bytes=VMEM_BYTES),
-        name=name,
     )(*operands)
 
 
-def local(state, source, absorption):
+def relaxation(state, source, absorption):
     space, slab = lax.axis_index("space"), lax.axis_index("tm")
     count, slabs = lax.axis_size("space"), lax.axis_size("tm")
     steps, depth, nx, ny = source.shape
@@ -246,32 +254,29 @@
     coarse_crossed = across(coarse)
     opens = pieces_of(opens, crossed)
 
-    h, v = call(
-        functools.partial(open_kernel, count), "open", [idx, *opens], [field] * 2, [field] * 5 + [(2, *field)]
-    )
+    h, v = call(functools.partial(open_kernel, count), [idx, *opens], [field] * 2, [field] * 5 + [(2, *field)])
     closes_crossed, v = lax.optimization_barrier((closes_crossed, v))
     closes = pieces_of(closes, closes_crossed)
     before, mine = call(
-        functools.partial(close_kernel, count),
-        "close",
-        [idx, h, v, *closes],
-        [field, half],
-        [field] * 5 + [(steps - 2, *field)],
+        functools.partial(close_kernel, count), [idx, h, v, *closes], [field, half], [field] * 5 + [(steps - 2, *field)]
     )
-    coarse_crossed, mine = lax.optimization_barrier((coarse_crossed, mine))
+    coarse_crossed, before = lax.optimization_barrier((coarse_crossed, before))
+    coarse = pieces_of(coarse, coarse_crossed)
     mine = next_slab(mine)
-    coarse = pieces_of(coarse, coarse_crossed)
+    (sources,) = call(functools.partial(sort_kernel, count), [idx, *coarse, *opens, *closes], [(steps + 1, *field)], [])
+    mine, sources = lax.optimization_barrier((mine, sources))
     other = partner(mine, "space", 1)
     relaxed, change, partial = call(
-        functools.partial(final_kernel, count),
-        "final",
-        [idx, h, before, mine, other, *coarse, *opens, *closes],
+        final_kernel,
+        [idx, h, before, sources, mine, other],
         [source.shape, (depth, nx, ny), (1, ny)],
-        [field] * 5 + [(steps, *field)] * 2,
+        [field] * 5 + [(steps, *field)],
     )
     residual = next_slab(change)
     bit = 1
     while bit < slabs:
+        if 2 * bit >= slabs:
+            residual, partial = lax.optimization_barrier((residual, partial))
         partial = partial + partner(partial, "tm", bit)
         bit *= 2
     return relaxed, residual[None], partial[0, 0]
@@ -279,7 +284,7 @@
 
 def solution(mesh):
     return jax.shard_map(
-        local,
+        relaxation,
         mesh=mesh,
         in_specs=(
             P("tm", "space", None, None),

time: 65.9 us -> 67.9 us (1.030)
  local copies, waits for them, and re-layouts: 1.74 us -> 3.53 us
  waiting for transfers between devices: 24.3 us -> 23.1 us
  other arithmetic: 0.62 us -> 1.53 us
    ppermute x2, waiting for transfers between devices: 5.54 us -> 3.36 us  [next_slab(): return lax.ppermute(value, 'tm', [(i, i + 1) for i in range(count - 1)])]
    slice x4 -> x3, local copies, waits for them, and re-layouts: 1.05 us -> 2.87 us  [the longest x2 1.96 us: relaxation(): closes, coarse = (source[2:], source[:1])]
    ppermute x13, waiting for transfers between devices: 18.8 us -> 19.8 us  [partner(): return lax.ppermute(value, axis, [(i, i ^ bit) for i in range(count)])]
    concatenate x1, other arithmetic: 0.03 us -> 0.93 us  [relaxation(): opens = jnp.concatenate([state[:1], absorption[None], source[1:2]], axis=0)]
    pallas_call x3 -> x4, Pallas kernels: 16.3 us -> 16.9 us  [call(): pl.pallas_call(kernel, out_shape=tuple((jax.ShapeDtypeStruct(shape, jnp.f...]
  transfers between devices with their start and end apart: 15 -> 15, of which waited for: 9 -> 9; matrix products, arithmetic and copies ran while one was open for 1% -> 2% of each run, Pallas kernels for 12% -> 13%
where the time goes in v3:
time: 67.9 us; the launch traced here: 67.6 us
  waiting for transfers between devices  23.1 us (34%)
  starting transfers between devices  21.9 us (32%)
  Pallas kernels  16.9 us (25%)
  local copies, waits for them, and re-layouts  3.53 us (5%)
  other arithmetic  1.53 us (2%)
  between operations  0.71 us (1%)
    ppermute x13, waiting for transfers between devices, partner(): return lax.ppermute(value, axis, [(i, i ^ bit) for i in range(count)])  19.8 us
    pallas_call x4, Pallas kernels, call(): pl.pallas_call(kernel, out_shape=tuple((jax.ShapeDtypeStruct(shape, jnp.f...  16.9 us
    ppermute x13, starting transfers between devices, partner(): return lax.ppermute(value, axis, [(i, i ^ bit) for i in range(count)])  14.1 us
    ppermute x2, starting transfers between devices, next_slab(): return lax.ppermute(value, 'tm', [(i, i + 1) for i in range(count - 1)])  7.8 us
    ppermute x2, waiting for transfers between devices, next_slab(): return lax.ppermute(value, 'tm', [(i, i + 1) for i in range(count - 1)])  3.36 us
    slice x2, local copies, waits for them, and re-layouts, relaxation(): closes, coarse = (source[2:], source[:1])  1.96 us
  transfers between devices with their start and end apart: 15, of which 9 were waited for; matrix products, arithmetic and copies ran while one was open for 2% of the time, Pallas kernels for 13%

profile of v3, /device:TPU:0, one launch (start us, length us, event | category | flops | bytes accessed | tf_op | source)
XLA Modules:
  0.0 67.6 jit_solution(5780701581996138718)
XLA Ops:
  0.6 0.9 %slice.15 = f32[1,4,64,128]{3,2,1,0:T(8,128)S(1)} slice(f32[4,4,64,128]{3,2,1,0:T(8,128)} %param.3), slice={[0:1], [0:4], [0:64], [0:128]} | slice | bytes 262144 | tf_op jit(solution)/shard_map/slice | solution.py:250
  1.5 1.0 %fusion = (f32[1,4,64,128]{3,2,1,0:T(8,128)S(1)}, f32[1,4,64,128]{3,2,1,0:T(8,128)S(1)}) fusion(f32[4,4,64,128]{3,2,1,0:T(8,128)} %param.4), kind=kLoop, calls=%fused_computation.2 | loop fusion | bytes 524288 | tf_op jit(solution)/shard_map/slice | solution.py:251
  2.5 0.9 %pad_maximum_fusion.refs_0_.refs_4_ = f32[3,4,64,128]{3,2,1,0:T(8,128)S(1)} fusion(f32[1,4,64,128]{3,2,1,0:T(8,128)S(1)} %get-tuple-element.34, f32[1,4,64,128]{3,2,1,0:T(8,128)} %bitcast.7, f32[1,4,64,128]{3,2,1,0:T(8,128)S(1)} %slice.15), kind=kLoop, calls=%fused_computation | loop fusion | flops 196608 | bytes 786432 | tf_op jit(solution)/shard_map/concatenate | solution.py:250
  3.5 3.1 %collective-permute-start.1 = (f32[3,4,64,128]{3,2,1,0:T(8,128)S(1)}, f32[3,4,64,128]{3,2,1,0:T(8,128)S(1)}, u32[]{:S(2)}, u32[]{:S(2)}) collective-permute-start(f32[3,4,64,128]{3,2,1,0:T(8,128)S(1)} %pad_maximum_fusion.refs_0_.refs_4_), channel_id=1, source_target_pairs={{0,2},{1,3},{2,0},{3,1},{4,6},{5,7},{6,4},{7,5},{8,10},{9,11},{10,... | collective-permute-start | bytes 1179656 | tf_op jit(solution)/shard_map/ppermute | solution.py:44
  6.5 0.0 collective-permute-start
  6.5 9.1 %collective-permute-done.1.refs_2_.refs_6_ = f32[3,4,64,128]{3,2,1,0:T(8,128)S(1)} collective-permute-done((f32[3,4,64,128]{3,2,1,0:T(8,128)S(1)}, f32[3,4,64,128]{3,2,1,0:T(8,128)S(1)}, u32[]{:S(2)}, u32[]{:S(2)}) %collective-permute-start.1) | collective-permute-done | bytes 393248 | tf_op jit(solution)/shard_map/ppermute | solution.py:44
  15.7 0.0 collective-permute-start.2
  15.7 1.0 %slice.18.refs_0_.refs_8_ = f32[2,4,64,128]{3,2,1,0:T(8,128)S(1)} slice(f32[4,4,64,128]{3,2,1,0:T(8,128)} %param.4), slice={[2:4], [0:4], [0:64], [0:128]} | slice | bytes 524288 | tf_op jit(solution)/shard_map/slice | solution.py:251
  16.6 1.8 %collective-permute-start.4 = (f32[2,4,64,128]{3,2,1,0:T(8,128)S(1)}, f32[2,4,64,128]{3,2,1,0:T(8,128)S(1)}, u32[]{:S(2)}, u32[]{:S(2)}) collective-permute-start(f32[2,4,64,128]{3,2,1,0:T(8,128)S(1)} %slice.18.refs_0_.refs_8_), channel_id=1, source_target_pairs={{0,2},{1,3},{2,0},{3,1},{4,6},{5,7},{6,4},{7,5},{8,10},{9,11},{10,... | collective-permute-start | bytes 786440 | tf_op jit(solution)/shard_map/ppermute | solution.py:44
  18.4 0.2 collective-permute-start.5
  18.7 0.1 pad_add_fusion.idx_ref
  18.7 0.0 collective-permute-done.refs_1_.refs_5_
  18.7 0.0 collective-permute-done.2.refs_3_.refs_7_
  18.7 4.0 %shard_map.58 = (f32[16,8,8,128]{3,2,1,0:T(8,128)S(1)}, f32[16,8,8,128]{3,2,1,0:T(8,128)S(1)}) custom-call(s32[2]{0:T(128)S(1)} %pad_add_fusion.idx_ref, f32[3,4,64,128]{3,2,1,0:T(8,128)S(1)} %pad_maximum_fusion.refs_0_.refs_4_, f32[3,4,64,128]{3,2,1,0:T(8,128)S(1)} %collective-permute-done.refs_1_.refs_5_, ...), custom_call_target="tpu_custom_call" | custom-call | tf_op jit(solution)/shard_map/pallas_call | solution.py:230
  22.7 2.7 %collective-permute-done.4.refs_2_.refs_10_ = f32[2,4,64,128]{3,2,1,0:T(8,128)S(1)} collective-permute-done((f32[2,4,64,128]{3,2,1,0:T(8,128)S(1)}, f32[2,4,64,128]{3,2,1,0:T(8,128)S(1)}, u32[]{:S(2)}, u32[]{:S(2)}) %collective-permute-start.4) | collective-permute-done | bytes 262176 | tf_op jit(solution)/shard_map/ppermute | solution.py:44
  25.4 0.0 collective-permute-start.6
  25.4 1.7 %collective-permute-start.3 = (f32[1,4,64,128]{3,2,1,0:T(8,128)S(1)}, f32[1,4,64,128]{3,2,1,0:T(8,128)S(1)}, u32[]{:S(2)}, u32[]{:S(2)}) collective-permute-start(f32[1,4,64,128]{3,2,1,0:T(8,128)S(1)} %get-tuple-element.33.refs_0_), channel_id=1, source_target_pairs={{0,2},{1,3},{2,0},{3,1},{4,6},{5,7},{6,4},{7,5},{8,10},{9,11},{10,... | collective-permute-start | bytes 393224 | tf_op jit(solution)/shard_map/ppermute | solution.py:44
  27.2 0.0 collective-permute-done.5.refs_1_.refs_9_
  27.2 0.0 collective-permute-done.6.refs_3_.refs_11_
  27.2 3.9 %shard_map.59 = (f32[16,8,8,128]{3,2,1,0:T(8,128)S(1)}, f32[8,8,8,128]{3,2,1,0:T(8,128)S(1)}) custom-call(s32[2]{0:T(128)S(1)} %pad_add_fusion.idx_ref, f32[16,8,8,128]{3,2,1,0:T(8,128)S(1)} %get-tuple-element.18.h_ref, f32[16,8,8,128]{3,2,1,0:T(8,128)S(1)} %get-tuple-element.20.v_ref, f32[2,4,64,128]{3,2,1,0:T(8,128)S(1)} %slice.18.refs_0_.refs_8_, ...), custom_call_target="tpu_custom_call" | custom-call | tf_op jit(solution)/shard_map/pallas_call | solution.py:230
  31.1 3.4 %collective-permute-start.7 = (f32[8,8,8,128]{3,2,1,0:T(8,128)S(1)}, f32[8,8,8,128]{3,2,1,0:T(8,128)S(1)}, u32[]{:S(2)}, u32[]{:S(2)}) collective-permute-start(f32[8,8,8,128]{3,2,1,0:T(8,128)S(1)} %get-tuple-element.24), channel_id=1, source_target_pairs={{0,4},{4,8},{8,12},{12,16},{16,20},{20,24},{24,28},{1,5},{5,9},{9,... | collective-permute-start | bytes 786440 | tf_op jit(solution)/shard_map/ppermute | solution.py:49
  34.5 0.1 collective-permute-start.8
  34.6 0.0 collective-permute-done.3.refs_2_
  34.6 0.5 collective-permute-start.9
  35.1 0.8 %collective-permute-done.8.refs_1_ = f32[1,4,64,128]{3,2,1,0:T(8,128)S(1)} collective-permute-done((f32[1,4,64,128]{3,2,1,0:T(8,128)S(1)}, f32[1,4,64,128]{3,2,1,0:T(8,128)S(1)}, u32[]{:S(2)}, u32[]{:S(2)}) %collective-permute-start.8) | collective-permute-done | bytes 131104 | tf_op jit(solution)/shard_map/ppermute | solution.py:44
  36.0 0.2 collective-permute-done.9.refs_3_
  36.1 1.0 %shard_map.60.s_ref = f32[5,16,8,8,128]{4,3,2,1,0:T(8,128)S(1)} custom-call(s32[2]{0:T(128)S(1)} %pad_add_fusion.idx_ref, f32[1,4,64,128]{3,2,1,0:T(8,128)S(1)} %get-tuple-element.33.refs_0_, f32[1,4,64,128]{3,2,1,0:T(8,128)S(1)} %collective-permute-done.8.refs_1_, f32[1,4,64,128]{3,2,1,0:T(8,128)S(1)} %collective-permute-done.3.refs_2_, ...), custom_call_target="tpu_custom_call" | custom-call | tf_op jit(solution)/shard_map/pallas_call | solution.py:230
  37.1 3.4 %collective-permute-done.7.mine_ref = f32[8,8,8,128]{3,2,1,0:T(8,128)S(1)} collective-permute-done((f32[8,8,8,128]{3,2,1,0:T(8,128)S(1)}, f32[8,8,8,128]{3,2,1,0:T(8,128)S(1)}, u32[]{:S(2)}, u32[]{:S(2)}) %collective-permute-start.7) | collective-permute-done | bytes 262176 | tf_op jit(solution)/shard_map/ppermute | solution.py:49
  40.5 0.0 collective-permute-start.10
  40.5 1.5 %collective-permute-done.10.other_ref = f32[8,8,8,128]{3,2,1,0:T(8,128)S(1)} collective-permute-done((f32[8,8,8,128]{3,2,1,0:T(8,128)S(1)}, f32[8,8,8,128]{3,2,1,0:T(8,128)S(1)}, u32[]{:S(2)}, u32[]{:S(2)}) %collective-permute-start.10) | collective-permute-done | bytes 262176 | tf_op jit(solution)/shard_map/ppermute | solution.py:44
  42.0 8.0 %shard_map.61 = (f32[4,4,64,128]{3,2,1,0:T(8,128)}, f32[4,64,128]{2,1,0:T(8,128)S(1)}, f32[1,128]{1,0:T(1,128)S(1)}) custom-call(s32[2]{0:T(128)S(1)} %pad_add_fusion.idx_ref, f32[16,8,8,128]{3,2,1,0:T(8,128)S(1)} %get-tuple-element.18.h_ref, f32[16,8,8,128]{3,2,1,0:T(8,128)S(1)} %get-tuple-element.23.before_ref, f32[5,16,8,8,128]{4,3,2,1,0:T(8,128)S(1)} %shard_map.60.s_ref, ...), custom_call_target="tpu_custom_call" | custom-call | tf_op jit(solution)/shard_map/pallas_call | solution.py:230
  50.0 4.4 %collective-permute-start.11 = (f32[4,64,128]{2,1,0:T(8,128)S(1)}, f32[4,64,128]{2,1,0:T(8,128)S(1)}, u32[]{:S(2)}, u32[]{:S(2)}) collective-permute-start(f32[4,64,128]{2,1,0:T(8,128)S(1)} %get-tuple-element.29), channel_id=1, source_target_pairs={{0,4},{4,8},{8,12},{12,16},{16,20},{20,24},{24,28},{1,5},{5,9},{9,... | collective-permute-start | bytes 393224 | tf_op jit(solution)/shard_map/ppermute | solution.py:49
  54.3 2.5 %collective-permute-start.12 = (f32[1,128]{1,0:T(1,128)S(1)}, f32[1,128]{1,0:T(1,128)S(1)}, u32[]{:S(2)}, u32[]{:S(2)}) collective-permute-start(f32[1,128]{1,0:T(1,128)S(1)} %get-tuple-element.30), channel_id=1, source_target_pairs={{0,4},{4,0},{8,12},{12,8},{16,20},{20,16},{24,28},{28,24},{1,5},{5... | collective-permute-start | bytes 1544 | tf_op jit(solution)/shard_map/ppermute | solution.py:44
  56.9 1.5 %collective-permute-done.12 = f32[1,128]{1,0:T(1,128)S(1)} collective-permute-done((f32[1,128]{1,0:T(1,128)S(1)}, f32[1,128]{1,0:T(1,128)S(1)}, u32[]{:S(2)}, u32[]{:S(2)}) %collective-permute-start.12) | collective-permute-done | bytes 544 | tf_op jit(solution)/shard_map/ppermute | solution.py:44
  58.4 1.6 %collective-permute-start.13 = (f32[1,128]{1,0:T(1,128)S(1)}, f32[1,128]{1,0:T(1,128)S(1)}, u32[]{:S(2)}, u32[]{:S(2)}) collective-permute-start(f32[1,128]{1,0:T(1,128)S(1)} %add.9), channel_id=1, source_target_pairs={{0,8},{4,12},{8,0},{12,4},{16,24},{20,28},{24,16},{28,20},{1,9},{5... | collective-permute-start | bytes 1544 | tf_op jit(solution)/shard_map/ppermute | solution.py:44
  60.0 2.0 %collective-permute-done.13 = f32[1,128]{1,0:T(1,128)S(1)} collective-permute-done((f32[1,128]{1,0:T(1,128)S(1)}, f32[1,128]{1,0:T(1,128)S(1)}, u32[]{:S(2)}, u32[]{:S(2)}) %collective-permute-start.13) | collective-permute-done | bytes 544 | tf_op jit(solution)/shard_map/ppermute | solution.py:44
  62.0 0.0 collective-permute-done.11
  62.0 2.6 %collective-permute-start.14 = (f32[1,128]{1,0:T(1,128)S(1)}, f32[1,128]{1,0:T(1,128)S(1)}, u32[]{:S(2)}, u32[]{:S(2)}) collective-permute-start(f32[1,128]{1,0:T(1,128)S(1)} %add.10), channel_id=1, source_target_pairs={{0,16},{4,20},{8,24},{12,28},{16,0},{20,4},{24,8},{28,12},{1,17},{... | collective-permute-start | bytes 1544 | tf_op jit(solution)/shard_map/ppermute | solution.py:44
  64.6 1.9 %collective-permute-done.14 = f32[1,128]{1,0:T(1,128)S(1)} collective-permute-done((f32[1,128]{1,0:T(1,128)S(1)}, f32[1,128]{1,0:T(1,128)S(1)}, u32[]{:S(2)}, u32[]{:S(2)}) %collective-permute-start.14) | collective-permute-done | bytes 544 | tf_op jit(solution)/shard_map/ppermute | solution.py:44
  66.5 0.5 add.11
  67.0 0.7 copy.7
  (2 shorter events, 0.0 us)
Async XLA Ops:
  3.5 12.2 %collective-permute-start.1 = (f32[3,4,64,128]{3,2,1,0:T(8,128)S(1)}, f32[3,4,64,128]{3,2,1,0:T(8,128)S(1)}, u32[]{:S(2)}, u32[]{:S(2)}) collective-permute-start(f32[3,4,64,128]{3,2,1,0:T(8,128)S(1)} %pad_maximum_fusion.refs_0_.refs_4_), channel_id=1, source_target_pairs={{0,2},{1,3},{2,0},{3,1},{4,6},{5,7},{6,4},{7,5},{8,10},{9,11},{10,... | collective-permute-start | bytes 1179656 | tf_op jit(solution)/shard_map/ppermute | solution.py:44
  6.5 12.2 %collective-permute-start = (f32[3,4,64,128]{3,2,1,0:T(8,128)S(1)}, f32[3,4,64,128]{3,2,1,0:T(8,128)S(1)}, u32[]{:S(2)}, u32[]{:S(2)}) collective-permute-start(f32[3,4,64,128]{3,2,1,0:T(8,128)S(1)} %pad_maximum_fusion.refs_0_.refs_4_), channel_id=1, source_target_pairs={{0,1},{1,0},{2,3},{3,2},{4,5},{5,4},{6,7},{7,6},{8,9},{9,8},{10,11... | collective-permute-start | bytes 1179656 | tf_op jit(solution)/shard_map/ppermute | solution.py:44
  15.7 3.1 %collective-permute-start.2 = (f32[3,4,64,128]{3,2,1,0:T(8,128)S(1)}, f32[3,4,64,128]{3,2,1,0:T(8,128)S(1)}, u32[]{:S(2)}, u32[]{:S(2)}) collective-permute-start(f32[3,4,64,128]{3,2,1,0:T(8,128)S(1)} %collective-permute-done.1.refs_2_.refs_6_), channel_id=1, source_target_pairs={{0,1},{1,0},{2,3},{3,2},{4,5},{5,4},{6,7},{7,6},{8,9},{9,8},{10,11... | collective-permute-start | bytes 1179656 | tf_op jit(solution)/shard_map/ppermute | solution.py:44
  16.6 8.8 %collective-permute-start.4 = (f32[2,4,64,128]{3,2,1,0:T(8,128)S(1)}, f32[2,4,64,128]{3,2,1,0:T(8,128)S(1)}, u32[]{:S(2)}, u32[]{:S(2)}) collective-permute-start(f32[2,4,64,128]{3,2,1,0:T(8,128)S(1)} %slice.18.refs_0_.refs_8_), channel_id=1, source_target_pairs={{0,2},{1,3},{2,0},{3,1},{4,6},{5,7},{6,4},{7,5},{8,10},{9,11},{10,... | collective-permute-start | bytes 786440 | tf_op jit(solution)/shard_map/ppermute | solution.py:44
  18.4 8.7 %collective-permute-start.5 = (f32[2,4,64,128]{3,2,1,0:T(8,128)S(1)}, f32[2,4,64,128]{3,2,1,0:T(8,128)S(1)}, u32[]{:S(2)}, u32[]{:S(2)}) collective-permute-start(f32[2,4,64,128]{3,2,1,0:T(8,128)S(1)} %slice.18.refs_0_.refs_8_), channel_id=1, source_target_pairs={{0,1},{1,0},{2,3},{3,2},{4,5},{5,4},{6,7},{7,6},{8,9},{9,8},{10,11... | collective-permute-start | bytes 786440 | tf_op jit(solution)/shard_map/ppermute | solution.py:44
  25.4 1.8 %collective-permute-start.6 = (f32[2,4,64,128]{3,2,1,0:T(8,128)S(1)}, f32[2,4,64,128]{3,2,1,0:T(8,128)S(1)}, u32[]{:S(2)}, u32[]{:S(2)}) collective-permute-start(f32[2,4,64,128]{3,2,1,0:T(8,128)S(1)} %collective-permute-done.4.refs_2_.refs_10_), channel_id=1, source_target_pairs={{0,1},{1,0},{2,3},{3,2},{4,5},{5,4},{6,7},{7,6},{8,9},{9,8},{10,11... | collective-permute-start | bytes 786440 | tf_op jit(solution)/shard_map/ppermute | solution.py:44
  25.4 9.2 %collective-permute-start.3 = (f32[1,4,64,128]{3,2,1,0:T(8,128)S(1)}, f32[1,4,64,128]{3,2,1,0:T(8,128)S(1)}, u32[]{:S(2)}, u32[]{:S(2)}) collective-permute-start(f32[1,4,64,128]{3,2,1,0:T(8,128)S(1)} %get-tuple-element.33.refs_0_), channel_id=1, source_target_pairs={{0,2},{1,3},{2,0},{3,1},{4,6},{5,7},{6,4},{7,5},{8,10},{9,11},{10,... | collective-permute-start | bytes 393224 | tf_op jit(solution)/shard_map/ppermute | solution.py:44
  31.1 9.3 %collective-permute-start.7 = (f32[8,8,8,128]{3,2,1,0:T(8,128)S(1)}, f32[8,8,8,128]{3,2,1,0:T(8,128)S(1)}, u32[]{:S(2)}, u32[]{:S(2)}) collective-permute-start(f32[8,8,8,128]{3,2,1,0:T(8,128)S(1)} %get-tuple-element.24), channel_id=1, source_target_pairs={{0,4},{4,8},{8,12},{12,16},{16,20},{20,24},{24,28},{1,5},{5,9},{9,... | collective-permute-start | bytes 786440 | tf_op jit(solution)/shard_map/ppermute | solution.py:49
  34.5 1.4 %collective-permute-start.8 = (f32[1,4,64,128]{3,2,1,0:T(8,128)S(1)}, f32[1,4,64,128]{3,2,1,0:T(8,128)S(1)}, u32[]{:S(2)}, u32[]{:S(2)}) collective-permute-start(f32[1,4,64,128]{3,2,1,0:T(8,128)S(1)} %get-tuple-element.33.refs_0_), channel_id=1, source_target_pairs={{0,1},{1,0},{2,3},{3,2},{4,5},{5,4},{6,7},{7,6},{8,9},{9,8},{10,11... | collective-permute-start | bytes 393224 | tf_op jit(solution)/shard_map/ppermute | solution.py:44
  34.6 1.5 %collective-permute-start.9 = (f32[1,4,64,128]{3,2,1,0:T(8,128)S(1)}, f32[1,4,64,128]{3,2,1,0:T(8,128)S(1)}, u32[]{:S(2)}, u32[]{:S(2)}) collective-permute-start(f32[1,4,64,128]{3,2,1,0:T(8,128)S(1)} %collective-permute-done.3.refs_2_), channel_id=1, source_target_pairs={{0,1},{1,0},{2,3},{3,2},{4,5},{5,4},{6,7},{7,6},{8,9},{9,8},{10,11... | collective-permute-start | bytes 393224 | tf_op jit(solution)/shard_map/ppermute | solution.py:44
  40.5 1.5 %collective-permute-start.10 = (f32[8,8,8,128]{3,2,1,0:T(8,128)S(1)}, f32[8,8,8,128]{3,2,1,0:T(8,128)S(1)}, u32[]{:S(2)}, u32[]{:S(2)}) collective-permute-start(f32[8,8,8,128]{3,2,1,0:T(8,128)S(1)} %collective-permute-done.7.mine_ref), channel_id=1, source_target_pairs={{0,1},{1,0},{2,3},{3,2},{4,5},{5,4},{6,7},{7,6},{8,9},{9,8},{10,11... | collective-permute-start | bytes 786440 | tf_op jit(solution)/shard_map/ppermute | solution.py:44
  50.0 12.0 %collective-permute-start.11 = (f32[4,64,128]{2,1,0:T(8,128)S(1)}, f32[4,64,128]{2,1,0:T(8,128)S(1)}, u32[]{:S(2)}, u32[]{:S(2)}) collective-permute-start(f32[4,64,128]{2,1,0:T(8,128)S(1)} %get-tuple-element.29), channel_id=1, source_target_pairs={{0,4},{4,8},{8,12},{12,16},{16,20},{20,24},{24,28},{1,5},{5,9},{9,... | collective-permute-start | bytes 393224 | tf_op jit(solution)/shard_map/ppermute | solution.py:49
  54.3 4.1 %collective-permute-start.12 = (f32[1,128]{1,0:T(1,128)S(1)}, f32[1,128]{1,0:T(1,128)S(1)}, u32[]{:S(2)}, u32[]{:S(2)}) collective-permute-start(f32[1,128]{1,0:T(1,128)S(1)} %get-tuple-element.30), channel_id=1, source_target_pairs={{0,4},{4,0},{8,12},{12,8},{16,20},{20,16},{24,28},{28,24},{1,5},{5... | collective-permute-start | bytes 1544 | tf_op jit(solution)/shard_map/ppermute | solution.py:44
  58.4 3.6 %collective-permute-start.13 = (f32[1,128]{1,0:T(1,128)S(1)}, f32[1,128]{1,0:T(1,128)S(1)}, u32[]{:S(2)}, u32[]{:S(2)}) collective-permute-start(f32[1,128]{1,0:T(1,128)S(1)} %add.9), channel_id=1, source_target_pairs={{0,8},{4,12},{8,0},{12,4},{16,24},{20,28},{24,16},{28,20},{1,9},{5... | collective-permute-start | bytes 1544 | tf_op jit(solution)/shard_map/ppermute | solution.py:44
  62.0 4.5 %collective-permute-start.14 = (f32[1,128]{1,0:T(1,128)S(1)}, f32[1,128]{1,0:T(1,128)S(1)}, u32[]{:S(2)}, u32[]{:S(2)}) collective-permute-start(f32[1,128]{1,0:T(1,128)S(1)} %add.10), channel_id=1, source_target_pairs={{0,16},{4,20},{8,24},{12,28},{16,0},{20,4},{24,8},{28,12},{1,17},{... | collective-permute-start | bytes 1544 | tf_op jit(solution)/shard_map/ppermute | solution.py:44
